TPU v7x, 512 devices: a whole 4x8x8 slice. The times are simulated.
512 devices in a mesh: gx: 64 (over x, z, y_hi), gy: 8 (over y_lo, core).
Axes of the slice: x: 4, y: 8 (y_hi: 2, y_lo: 4; y = y_hi * 4 + y_lo), z: 8, core: 2. Of those that a mesh axis runs over, the one named last changes fastest.
Arguments:
- moisture_ratio: float32 [2, 512, 1024], P(None, 'gx', 'gy'), may hold values from 11 to 14
- kelvin_warmth: float32 [2, 512, 1024], P(None, 'gx', 'gy'), may hold values from 286 to 292
- droplet_size_micron: float32 [8, 2, 512, 1024], P(None, None, 'gx', 'gy'), may hold values from 0.5 to 25
- weighting_factor: float32 [8, 2, 512, 1024], P(None, None, 'gx', 'gy'), may hold values from 0.1 to 2
- dry_nucleus_size: float32 [8, 2, 512, 1024], P(None, None, 'gx', 'gy'), may hold values from 0.02 to 0.3
- fractional_offset_east: float32 [8, 2, 512, 1024], P(None, None, 'gx', 'gy'), may hold values from 0 to 1
- fractional_offset_north: float32 [8, 2, 512, 1024], P(None, None, 'gx', 'gy'), may hold values from 0 to 1
- encounter_permutation: int32 [8, 2, 512, 1024], P(None, None, 'gx', 'gy'), may hold values from 0 to 7, as said below
- departing_eastwest_lists: int32 [64, 2, 8192], P('gx', None, 'gy'), may hold values from -1 to 16383, as said below
- departing_northsouth_lists: int32 [64, 2, 384], P('gx', None, 'gy'), may hold values from -1 to 16383, as said below
- departing_diagonal_lists: int32 [64, 4, 64], P('gx', None, 'gy'), may hold values from -1 to 16383, as said below
Outputs:
- resulting_moisture_ratio: float32 [2, 512, 1024], P(None, 'gx', 'gy')
- resulting_kelvin_value: float32 [2, 512, 1024], P(None, 'gx', 'gy')
- resulting_droplet_size: float32 [8, 2, 512, 1024], P(None, None, 'gx', 'gy')
- resulting_weighting_factor: float32 [8, 2, 512, 1024], P(None, None, 'gx', 'gy')
- arrival_particle_records: float32 [5, 64, 17408], P(None, 'gx', 'gy')
- arrival_box_index: int32 [64, 17408], P('gx', 'gy')
Inputs may be any that keep to these rules, and one draw needn't show every extreme that they name: `encounter_permutation`: along the first dimension, the 8 entries of each cell are a permutation of 0 to 7. `departing_eastwest_lists`: each list holds live slot numbers of its own device first and -1 after them, at most 1024 live, and some list of some device is full. Row 0 names only droplets of cells with i = 7, row 1 only i = 0, both only 0 < j < 127. No slot is named twice among all lists of a device. `departing_northsouth_lists`: each list holds live slot numbers of its own device first and -1 after them, at most 48 live, and some list of some device is full. Row 0 names only droplets of cells with j = 127, row 1 only j = 0, both only 0 < i < 7. `departing_diagonal_lists`: each list holds live slot numbers of its own device first and -1 after them, at most 8 live, and some list of some device is full. Row r names only droplets of the corner cell that its move points to: i = 7 for rows 0 and 1, i = 0 for rows 2 and 3, j = 127 for rows 0 and 2, j = 0 for rows 1 and 3.
All inputs are finite; a program needn't handle non-finite values.
Results may differ from a plain program's by a relative error of at most 0.0003.
Values sent between devices are 32-bit elements; how exact they have to be, the bound alone decides.
No kernel may reach another device: no remote copies, remote signals or barrier semaphores. Data moves between devices by JAX's collectives and lax.ppermute only.
A program may use at most 64 MiB of HBM per device.

v0:
```python
import jax
import jax.numpy as jnp
from jax import lax
from jax.sharding import PartitionSpec as P

NEWTON = 4


MIX_HORIZONTAL = 0.2
MIX_VERTICAL = 0.05
EXCESS_FACTOR = 4.2222
CURVATURE = 0.0012
KAPPA_SOLUTE = 0.6
GROWTH_STEP = 200.0
COLLIDE_RATE = 4e-07
VAPOUR_PER_SOURCE = 0.001
WARMING_FACTOR = 0.00249


def with_halo(block, sides, width):
    for axis, dim in sides:
        count = lax.axis_size(axis)
        forward = [(i, i + 1) for i in range(count - 1)]
        forward.append((count - 1, 0))
        backward = [(target, source) for source, target in forward]
        low = lax.ppermute(
            lax.slice_in_dim(block, block.shape[dim] - width, None, axis=dim), axis, forward
        )
        high = lax.ppermute(lax.slice_in_dim(block, 0, width, axis=dim), axis, backward)
        block = jnp.concatenate([low, block, high], axis=dim)
    return block


def moisture_excess(moisture_ratio, kelvin_warmth):
    maximum_list_length = EXCESS_FACTOR * jnp.exp(
        17.27 * (kelvin_warmth - 273.15) / (kelvin_warmth - 35.86)
    )
    return moisture_ratio / maximum_list_length - 1.0


def kernel_weights(offset):
    return (
        jnp.maximum(0.5 - offset, 0.0),
        1.0 - jnp.abs(offset - 0.5),
        jnp.maximum(offset - 0.5, 0.0),
    )


def vertical_mix(centre, level_axis):
    levels = centre.shape[level_axis]
    above = jnp.concatenate(
        [
            lax.slice_in_dim(centre, 1, levels, axis=level_axis),
            lax.slice_in_dim(centre, levels - 1, levels, axis=level_axis),
        ],
        level_axis,
    )
    below = jnp.concatenate(
        [
            lax.slice_in_dim(centre, 0, 1, axis=level_axis),
            lax.slice_in_dim(centre, 0, levels - 1, axis=level_axis),
        ],
        level_axis,
    )
    return above + below - 2.0 * centre


def mix_padded(padded):
    centre = padded[:, :, 1:-1, 1:-1]
    horizontal = (
        padded[:, :, 2:, 1:-1]
        + padded[:, :, :-2, 1:-1]
        + padded[:, :, 1:-1, 2:]
        + padded[:, :, 1:-1, :-2]
        - 4.0 * centre
    )
    return centre + MIX_HORIZONTAL * horizontal + MIX_VERTICAL * vertical_mix(centre, 1)


def grow_droplets(droplet_size_micron, dry_nucleus_size, forcing):
    initial = droplet_size_micron * droplet_size_micron
    solute = KAPPA_SOLUTE * dry_nucleus_size * dry_nucleus_size * dry_nucleus_size
    lowest = dry_nucleus_size * dry_nucleus_size
    wetted = initial
    for sweep in range(NEWTON):
        root_wet = jnp.sqrt(wetted)
        inverse = 1.0 / (wetted * root_wet)
        residue = wetted - initial - GROWTH_STEP * (forcing + solute * inverse)
        slope_value = 1.0 + 1.5 * GROWTH_STEP * solute * inverse / wetted
        wetted = jnp.maximum(wetted - residue / slope_value, lowest)
    return wetted


def select_member(values, order_row):
    total = jnp.zeros_like(values[0])
    for member in range(values.shape[0]):
        total = total + jnp.where(order_row == member, values[member], 0.0)
    return total


def coalesce(grown_radius, weighting_factor, encounter_permutation):
    members = encounter_permutation.shape[0]
    new_radius = []
    new_mult = []
    for pair in range(members // 2):
        first_order = encounter_permutation[2 * pair]
        second_order = encounter_permutation[2 * pair + 1]
        first_radius = select_member(grown_radius, first_order)
        second_radius = select_member(grown_radius, second_order)
        first_mult = select_member(weighting_factor, first_order)
        second_mult = select_member(weighting_factor, second_order)
        first_big = first_mult >= second_mult
        high_radius = jnp.where(first_big, first_radius, second_radius)
        low_radius = jnp.where(first_big, second_radius, first_radius)
        high_mult = jnp.where(first_big, first_mult, second_mult)
        low_mult = jnp.where(first_big, second_mult, first_mult)
        radius_sum = first_radius + second_radius
        kernel = (
            COLLIDE_RATE
            * high_mult
            * radius_sum
            * radius_sum
            * jnp.abs(first_radius * first_radius - second_radius * second_radius)
        )
        chance = 1.0 - jnp.exp(-kernel)
        merged_radius = jnp.cbrt(
            low_radius * low_radius * low_radius + chance * high_radius * high_radius * high_radius
        )
        reduced_mult = high_mult - chance * low_mult
        new_radius.append(jnp.where(first_big, high_radius, merged_radius))
        new_radius.append(jnp.where(first_big, merged_radius, high_radius))
        new_mult.append(jnp.where(first_big, reduced_mult, low_mult))
        new_mult.append(jnp.where(first_big, low_mult, reduced_mult))
    out_radius = []
    out_mult = []
    for target in range(members):
        radius_total = jnp.zeros_like(grown_radius[0])
        mult_total = jnp.zeros_like(grown_radius[0])
        for position in range(members):
            hit = encounter_permutation[position] == target
            radius_total = radius_total + jnp.where(hit, new_radius[position], 0.0)
            mult_total = mult_total + jnp.where(hit, new_mult[position], 0.0)
        out_radius.append(radius_total)
        out_mult.append(mult_total)
    return (jnp.stack(out_radius, 0), jnp.stack(out_mult, 0))


def make_records(fields, lists, directions, cells_x, cells_y, levels):
    list_rows = lists.shape[0]
    list_length = lists.shape[1]
    is_live = lists >= 0
    safe_slot = jnp.where(is_live, lists, 0)
    flat_index = safe_slot.reshape(-1)
    picked = jnp.stack(
        [jnp.take(single, flat_index).reshape(list_rows, list_length) for single in fields], 1
    )
    picked = jnp.where(is_live[:, None, :], picked, 0.0)
    cell_index = safe_slot % (levels * cells_x * cells_y)
    level_index = cell_index // (cells_x * cells_y)
    index_x = cell_index // cells_y % cells_x
    index_y = cell_index % cells_y
    move_x = jnp.array([entry[0] for entry in directions], jnp.int32).reshape(list_rows, 1)
    move_y = jnp.array([entry[1] for entry in directions], jnp.int32).reshape(list_rows, 1)
    target = (level_index * cells_x + (index_x + move_x) % cells_x) * cells_y + (
        index_y + move_y
    ) % cells_y
    target = jnp.where(is_live, target, -1).astype(jnp.float32)
    return jnp.concatenate([picked, target[:, None, :]], 1)


def per_device(
    moisture_ratio,
    kelvin_warmth,
    droplet_size_micron,
    weighting_factor,
    dry_nucleus_size,
    fractional_offset_east,
    fractional_offset_north,
    encounter_permutation,
    departing_eastwest_lists,
    departing_northsouth_lists,
    departing_diagonal_lists,
):
    levels = moisture_ratio.shape[0]
    cells_x = moisture_ratio.shape[1]
    cells_y = moisture_ratio.shape[2]
    atmosphere_state_arrays = jnp.stack([moisture_ratio, kelvin_warmth])
    wide_fields = with_halo(atmosphere_state_arrays, (("gx", 2), ("gy", 3)), 2)
    mixed_wide = mix_padded(wide_fields)
    humid_ext = moisture_excess(mixed_wide[0], mixed_wide[1])
    stirred_state_arrays = mixed_wide[:, :, 1:-1, 1:-1]
    weight_x = kernel_weights(fractional_offset_east)
    weight_y = kernel_weights(fractional_offset_north)
    forcing = jnp.zeros_like(droplet_size_micron)
    for shift_x in range(3):
        for shift_y in range(3):
            window = humid_ext[:, shift_x : shift_x + cells_x, shift_y : shift_y + cells_y]
            forcing = forcing + weight_x[shift_x] * weight_y[shift_y] * window[None]
    forcing = forcing - CURVATURE / droplet_size_micron
    wetted = grow_droplets(droplet_size_micron, dry_nucleus_size, forcing)
    condensed = weighting_factor * (
        wetted * jnp.sqrt(wetted) - droplet_size_micron * droplet_size_micron * droplet_size_micron
    )
    source_ext = jnp.zeros((levels, cells_x + 2, cells_y + 2), jnp.float32)
    for shift_x in range(3):
        for shift_y in range(3):
            deposit = jnp.sum(weight_x[shift_x] * weight_y[shift_y] * condensed, axis=0)
            source_ext = source_ext.at[
                :, shift_x : shift_x + cells_x, shift_y : shift_y + cells_y
            ].add(deposit)
    rim_values = with_halo(source_ext, (("gx", 1), ("gy", 2)), 1)
    accumulated_deposition = source_ext[:, 1:-1, 1:-1]
    accumulated_deposition = accumulated_deposition.at[:, 0, :].add(
        rim_values[:, 0, 2 : cells_y + 2]
    )
    accumulated_deposition = accumulated_deposition.at[:, cells_x - 1, :].add(
        rim_values[:, cells_x + 3, 2 : cells_y + 2]
    )
    accumulated_deposition = accumulated_deposition.at[:, :, 0].add(
        rim_values[:, 2 : cells_x + 2, 0]
    )
    accumulated_deposition = accumulated_deposition.at[:, :, cells_y - 1].add(
        rim_values[:, 2 : cells_x + 2, cells_y + 3]
    )
    accumulated_deposition = accumulated_deposition.at[:, 0, 0].add(rim_values[:, 0, 0])
    accumulated_deposition = accumulated_deposition.at[:, cells_x - 1, 0].add(
        rim_values[:, cells_x + 3, 0]
    )
    accumulated_deposition = accumulated_deposition.at[:, 0, cells_y - 1].add(
        rim_values[:, 0, cells_y + 3]
    )
    accumulated_deposition = accumulated_deposition.at[:, cells_x - 1, cells_y - 1].add(
        rim_values[:, cells_x + 3, cells_y + 3]
    )
    resulting_moisture_ratio = stirred_state_arrays[0] - VAPOUR_PER_SOURCE * accumulated_deposition
    resulting_kelvin_value = stirred_state_arrays[1] + WARMING_FACTOR * accumulated_deposition
    grown_radius = jnp.sqrt(wetted)
    resulting_droplet_size, coalesced = coalesce(
        grown_radius, weighting_factor, encounter_permutation
    )
    lists_x = departing_eastwest_lists[0]
    lists_y = departing_northsouth_lists[0]
    lists_corner = departing_diagonal_lists[0]
    slot_count = droplet_size_micron.size
    all_lists = jnp.concatenate(
        [lists_x.reshape(-1), lists_y.reshape(-1), lists_corner.reshape(-1)]
    )
    departed = (
        jnp.zeros((slot_count,), jnp.float32)
        .at[jnp.where(all_lists >= 0, all_lists, slot_count)]
        .set(1.0, mode="drop")
    )
    resulting_weighting_factor = jnp.where(
        departed.reshape(droplet_size_micron.shape) > 0.0, 0.0, coalesced
    )
    fields = (
        resulting_droplet_size.reshape(-1),
        coalesced.reshape(-1),
        dry_nucleus_size.reshape(-1),
        fractional_offset_east.reshape(-1),
        fractional_offset_north.reshape(-1),
    )
    records_x = make_records(fields, lists_x, ((1, 0), (-1, 0)), cells_x, cells_y, levels)
    records_y = make_records(fields, lists_y, ((0, 1), (0, -1)), cells_x, cells_y, levels)
    records_corner = make_records(
        fields, lists_corner, ((1, 1), (1, -1), (-1, 1), (-1, -1)), cells_x, cells_y, levels
    )
    length_x = lists_x.shape[1]
    length_y = lists_y.shape[1]
    length_corner = lists_corner.shape[1]
    east_row = jnp.concatenate([records_x[0], records_corner[0], records_corner[1]], 1)
    west_row = jnp.concatenate([records_x[1], records_corner[2], records_corner[3]], 1)
    got_x = with_halo(jnp.stack([west_row, east_row], 1), (("gx", 1),), 1)
    from_west = got_x[:, 0]
    from_east = got_x[:, 3]
    north_row = jnp.concatenate(
        [
            records_y[0],
            from_west[:, length_x : length_x + length_corner],
            from_east[:, length_x : length_x + length_corner],
        ],
        1,
    )
    south_row = jnp.concatenate(
        [
            records_y[1],
            from_west[:, length_x + length_corner :],
            from_east[:, length_x + length_corner :],
        ],
        1,
    )
    got_y = with_halo(jnp.stack([south_row, north_row], 1), (("gy", 1),), 1)
    from_south = got_y[:, 0]
    from_north = got_y[:, 3]
    south_west = from_south[:, length_y : length_y + length_corner]
    south_east = from_south[:, length_y + length_corner :]
    north_west = from_north[:, length_y : length_y + length_corner]
    north_east = from_north[:, length_y + length_corner :]
    arrivals = jnp.concatenate(
        [
            from_west[:, :length_x],
            from_east[:, :length_x],
            from_south[:, :length_y],
            from_north[:, :length_y],
            south_west,
            south_east,
            north_west,
            north_east,
        ],
        1,
    )
    arrival_particle_records = arrivals[:5][:, None, :]
    arrival_box_index = arrivals[5].astype(jnp.int32)[None, :]
    return (
        resulting_moisture_ratio,
        resulting_kelvin_value,
        resulting_droplet_size,
        resulting_weighting_factor,
        arrival_particle_records,
        arrival_box_index,
    )


def solution(mesh):
    placed = (
        P(None, "gx", "gy"),
        P(None, "gx", "gy"),
        P(None, None, "gx", "gy"),
        P(None, None, "gx", "gy"),
        P(None, None, "gx", "gy"),
        P(None, None, "gx", "gy"),
        P(None, None, "gx", "gy"),
        P(None, None, "gx", "gy"),
        P("gx", None, "gy"),
        P("gx", None, "gy"),
        P("gx", None, "gy"),
    )
    return jax.shard_map(
        per_device,
        mesh=mesh,
        in_specs=placed,
        out_specs=(
            P(None, "gx", "gy"),
            P(None, "gx", "gy"),
            P(None, None, "gx", "gy"),
            P(None, None, "gx", "gy"),
            P(None, "gx", "gy"),
            P("gx", "gy"),
        ),
        check_vma=False,
    )
```

profile of v0, /device:TPU:25, one launch (start us, length us, event | category | flops | bytes accessed | tf_op | source)
XLA Modules:
  0.0 184.8 jit_solution(11689962978052684547)
XLA Ops:
  1.4 15.4 %collective-permute-start.1 = (f32[2,2,2,128]{3,2,1,0:T(2,128)S(1)}, f32[2,2,2,128]{3,2,1,0:T(2,128)S(1)}, u32[]{:S(2)}, u32[]{:S(2)}) collective-permute-start(f32[2,2,2,128]{3,2,1,0:T(2,128)S(1)} %get-tuple-element.362), channel_id=1, source_target_pairs={{8,0},{16,8},{24,16},{32,24},{40,32},{48,40},{56,48},{64,56},{72,6... | collective-permute-start | bytes 12296 | tf_op jit(solution)/shard_map/ppermute | solution.py:29
  16.9 2.1 %collective-permute-start = (f32[2,2,2,128]{3,2,1,0:T(2,128)S(1)}, f32[2,2,2,128]{3,2,1,0:T(2,128)S(1)}, u32[]{:S(2)}, u32[]{:S(2)}) collective-permute-start(f32[2,2,2,128]{3,2,1,0:T(2,128)S(1)} %get-tuple-element.361), channel_id=1, source_target_pairs={{0,8},{8,16},{16,24},{24,32},{32,40},{40,48},{48,56},{56,64},{64,7... | collective-permute-start | bytes 12296 | tf_op jit(solution)/shard_map/ppermute | solution.py:26
  23.1 11.2 %scatter_custom_fusion = f32[16384]{0:T(1024)S(1)} fusion(s32[2176]{0:T(1024)S(1)} %fusion.49, f32[2176]{0:T(1024)S(1)} %broadcast.4733, f32[]{:T(128)} %constant.715.clone.1), kind=kCustom, calls=%fused_computation.150 | custom fusion | bytes 65540 | tf_op jit(solution)/shard_map/scatter | solution.py:251
  35.1 11.8 %gather_fusion.4 = f32[2048]{0:T(1024)S(1)} fusion(f32[16384]{0:T(1024)S(1)} %bitcast.96, s32[2048]{0:T(1024)S(1)} %fusion.93), kind=kCustom, calls=%fused_computation.6.clone | custom fusion | bytes 24576 | tf_op jit(solution)/shard_map/jit(_take)/gather | solution.py:155
  48.3 11.8 %gather_fusion.2 = f32[2048]{0:T(1024)S(1)} fusion(f32[16384]{0:T(1024)S(1)} %bitcast.105, s32[2048]{0:T(1024)S(1)} %fusion.93), kind=kCustom, calls=%fused_computation.4.clone | custom fusion | bytes 24576 | tf_op jit(solution)/shard_map/jit(_take)/gather | solution.py:155
  61.6 5.4 %collective-permute-start.2 = (f32[2,2,12,2]{3,2,1,0:T(8,128)S(1)}, f32[2,2,12,2]{3,2,1,0:T(8,128)S(1)}, u32[]{:S(2)}, u32[]{:S(2)}) collective-permute-start(f32[2,2,12,2]{3,2,1,0:T(8,128)S(1)} %get-tuple-element.360), channel_id=1, source_target_pairs={{0,1},{1,2},{2,3},{3,4},{4,5},{5,6},{6,7},{7,0},{8,9},{9,10},{10,1... | collective-permute-start | bytes 1160 | tf_op jit(solution)/shard_map/ppermute | solution.py:26
  67.0 1.9 %collective-permute-start.3 = (f32[2,2,12,2]{3,2,1,0:T(8,128)S(1)}, f32[2,2,12,2]{3,2,1,0:T(8,128)S(1)}, u32[]{:S(2)}, u32[]{:S(2)}) collective-permute-start(f32[2,2,12,2]{3,2,1,0:T(8,128)S(1)} %get-tuple-element.359), channel_id=1, source_target_pairs={{1,0},{2,1},{3,2},{4,3},{5,4},{6,5},{7,6},{0,7},{9,8},{10,9},{11,1... | collective-permute-start | bytes 1160 | tf_op jit(solution)/shard_map/ppermute | solution.py:29
  68.9 11.8 %gather_fusion.3 = f32[2048]{0:T(1024)S(1)} fusion(f32[16384]{0:T(1024)S(1)} %bitcast.99, s32[2048]{0:T(1024)S(1)} %fusion.93), kind=kCustom, calls=%fused_computation.5.clone | custom fusion | bytes 24576 | tf_op jit(solution)/shard_map/jit(_take)/gather | solution.py:155
  88.5 2.2 %scatter-add.59 = f32[2,10,130]{2,1,0:T(8,128)S(1)} dynamic-update-slice(f32[2,10,130]{2,1,0:T(8,128)S(1)} %scatter-add.56, f32[2,8,128]{2,1,0:T(8,128)S(1)} %fusion.52, s32[]{:T(128)} %constant.752.clone, s32[]{:T(128)} %bitcast.4, s32[]{:T(128)} %bitcast.5) | dynamic-update-slice | bytes 16388 | tf_op jit(solution)/shard_map/scatter-add | solution.py:210
  90.7 2.0 %add_select_fusion = f32[2,8,128]{2,1,0:T(8,128)S(1)} fusion(f32[2,8,128]{2,1,0:T(8,128)S(1)} %get-tuple-element.231, f32[2,10,130]{2,1,0:T(8,128)S(1)} %scatter-add.59, s32[]{:T(128)} %bitcast.6, s32[]{:T(128)} %bitcast.7, pred[]{:T(512)} %and_reduce_fusion.1), kind=kLoop, calls=%fused_computation.183 | loop fusion | flops 4096 | bytes 24585 | tf_op jit(solution)/shard_map/select.19
  92.8 2.2 %scatter-add.60 = f32[2,10,130]{2,1,0:T(8,128)S(1)} dynamic-update-slice(f32[2,10,130]{2,1,0:T(8,128)S(1)} %scatter-add.59, f32[2,8,128]{2,1,0:T(8,128)S(1)} %add_select_fusion, s32[]{:T(128)} %constant.752.clone, s32[]{:T(128)} %bitcast.6, s32[]{:T(128)} %bitcast.7) | dynamic-update-slice | bytes 16388 | tf_op jit(solution)/shard_map/scatter-add | solution.py:210
  100.5 11.8 %gather_fusion.1 = f32[2048]{0:T(1024)S(1)} fusion(f32[16384]{0:T(1024)S(1)} %bitcast.102, s32[2048]{0:T(1024)S(1)} %fusion.93), kind=kCustom, calls=%fused_computation.3.clone | custom fusion | bytes 24576 | tf_op jit(solution)/shard_map/jit(_take)/gather | solution.py:155
  113.3 11.8 %gather_fusion = f32[2048]{0:T(1024)S(1)} fusion(f32[16384]{0:T(1024)S(1)} %bitcast.108, s32[2048]{0:T(1024)S(1)} %fusion.93), kind=kCustom, calls=%fused_computation.clone | custom fusion | bytes 24576 | tf_op jit(solution)/shard_map/jit(_take)/gather | solution.py:155
  128.1 1.9 %collective-permute-start.4 = (f32[2,1,130]{2,1,0:T(1,128)S(1)}, f32[2,1,130]{2,1,0:T(1,128)S(1)}, u32[]{:S(2)}, u32[]{:S(2)}) collective-permute-start(f32[2,1,130]{2,1,0:T(1,128)S(1)} %get-tuple-element.349), channel_id=1, source_target_pairs={{0,8},{8,16},{16,24},{24,32},{32,40},{40,48},{48,56},{56,64},{64,7... | collective-permute-start | bytes 3128 | tf_op jit(solution)/shard_map/ppermute | solution.py:26
  130.0 11.8 %collective-permute-start.5 = (f32[2,1,130]{2,1,0:T(1,128)S(1)}, f32[2,1,130]{2,1,0:T(1,128)S(1)}, u32[]{:S(2)}, u32[]{:S(2)}) collective-permute-start(f32[2,1,130]{2,1,0:T(1,128)S(1)} %get-tuple-element.348), channel_id=1, source_target_pairs={{8,0},{16,8},{24,16},{32,24},{40,32},{48,40},{56,48},{64,56},{72,6... | collective-permute-start | bytes 3128 | tf_op jit(solution)/shard_map/ppermute | solution.py:29
  143.2 1.9 %collective-permute-start.8 = (f32[6,1,1040]{2,0,1:T(8,128)S(1)}, f32[6,1,1040]{2,0,1:T(8,128)S(1)}, u32[]{:S(2)}, u32[]{:S(2)}) collective-permute-start(f32[6,1,1040]{2,0,1:T(8,128)S(1)} %bitcast.127), channel_id=1, source_target_pairs={{0,8},{8,16},{16,24},{24,32},{32,40},{40,48},{48,56},{56,64},{64,7... | collective-permute-start | bytes 74888 | tf_op jit(solution)/shard_map/ppermute | solution.py:26
  145.2 11.5 %collective-permute-start.9 = (f32[6,1,1040]{2,0,1:T(8,128)S(1)}, f32[6,1,1040]{2,0,1:T(8,128)S(1)}, u32[]{:S(2)}, u32[]{:S(2)}) collective-permute-start(f32[6,1,1040]{2,0,1:T(8,128)S(1)} %bitcast.128), channel_id=1, source_target_pairs={{8,0},{16,8},{24,16},{32,24},{40,32},{48,40},{56,48},{64,56},{72,6... | collective-permute-start | bytes 74888 | tf_op jit(solution)/shard_map/ppermute | solution.py:29
  157.3 6.3 %collective-permute-start.6 = (f32[2,12,1]{2,1,0:T(8,128)S(1)}, f32[2,12,1]{2,1,0:T(8,128)S(1)}, u32[]{:S(2)}, u32[]{:S(2)}) collective-permute-start(f32[2,12,1]{2,1,0:T(8,128)S(1)} %get-tuple-element.347), channel_id=1, source_target_pairs={{0,1},{1,2},{2,3},{3,4},{4,5},{5,6},{6,7},{7,0},{8,9},{9,10},{10,1... | collective-permute-start | bytes 296 | tf_op jit(solution)/shard_map/ppermute | solution.py:26
  163.6 1.9 %collective-permute-start.7 = (f32[2,12,1]{2,1,0:T(8,128)S(1)}, f32[2,12,1]{2,1,0:T(8,128)S(1)}, u32[]{:S(2)}, u32[]{:S(2)}) collective-permute-start(f32[2,12,1]{2,1,0:T(8,128)S(1)} %get-tuple-element.346), channel_id=1, source_target_pairs={{1,0},{2,1},{3,2},{4,3},{5,4},{6,5},{7,6},{0,7},{9,8},{10,9},{11,1... | collective-permute-start | bytes 296 | tf_op jit(solution)/shard_map/ppermute | solution.py:29
  165.8 4.6 %collective-permute-done.7 = f32[2,12,1]{2,1,0:T(8,128)S(1)} collective-permute-done((f32[2,12,1]{2,1,0:T(8,128)S(1)}, f32[2,12,1]{2,1,0:T(8,128)S(1)}, u32[]{:S(2)}, u32[]{:S(2)}) %collective-permute-start.7) | collective-permute-done | bytes 128 | tf_op jit(solution)/shard_map/ppermute | solution.py:29
  170.8 1.9 %broadcast_select_fusion.9 = f32[2,1,1]{2,1,0:T(1,128)S(1)} fusion(pred[]{:T(512)} %and_reduce_fusion, f32[2,12,1]{2,1,0:T(8,128)S(1)} %collective-permute-done.7, f32[2,8,128]{2,1,0:T(8,128)S(1)} %scatter-add.80, s32[]{:T(128)} %bitcast.8, s32[]{:T(128)} %bitcast.9), kind=kLoop, calls=%fused_computation.417 | loop fusion | flops 4 | bytes 33 | tf_op jit(solution)/shard_map/select.32
  174.7 1.9 %collective-permute-start.10 = (f32[6,1,64]{2,0,1:T(8,128)S(1)}, f32[6,1,64]{2,0,1:T(8,128)S(1)}, u32[]{:S(2)}, u32[]{:S(2)}) collective-permute-start(f32[6,1,64]{2,0,1:T(8,128)S(1)} %maximum_bitcast_fusion), channel_id=1, source_target_pairs={{0,1},{1,2},{2,3},{3,4},{4,5},{5,6},{6,7},{7,0},{8,9},{9,10},{10,1... | collective-permute-start | bytes 4616 | tf_op jit(solution)/shard_map/ppermute | solution.py:26
  176.7 2.4 %collective-permute-start.11 = (f32[6,1,64]{2,0,1:T(8,128)S(1)}, f32[6,1,64]{2,0,1:T(8,128)S(1)}, u32[]{:S(2)}, u32[]{:S(2)}) collective-permute-start(f32[6,1,64]{2,0,1:T(8,128)S(1)} %maximum_bitcast_fusion.1), channel_id=1, source_target_pairs={{1,0},{2,1},{3,2},{4,3},{5,4},{6,5},{7,6},{0,7},{9,8},{10,9},{11,1... | collective-permute-start | bytes 4616 | tf_op jit(solution)/shard_map/ppermute | solution.py:29
  179.8 3.6 %collective-permute-done.11 = f32[6,1,64]{2,0,1:T(8,128)S(1)} collective-permute-done((f32[6,1,64]{2,0,1:T(8,128)S(1)}, f32[6,1,64]{2,0,1:T(8,128)S(1)}, u32[]{:S(2)}, u32[]{:S(2)}) %collective-permute-start.11) | collective-permute-done | bytes 1568 | tf_op jit(solution)/shard_map/ppermute | solution.py:29
  (193 shorter events, 32.3 us)
Async XLA Ops:
  1.4 60.0 %collective-permute-start.1 = (f32[2,2,2,128]{3,2,1,0:T(2,128)S(1)}, f32[2,2,2,128]{3,2,1,0:T(2,128)S(1)}, u32[]{:S(2)}, u32[]{:S(2)}) collective-permute-start(f32[2,2,2,128]{3,2,1,0:T(2,128)S(1)} %get-tuple-element.362), channel_id=1, source_target_pairs={{8,0},{16,8},{24,16},{32,24},{40,32},{48,40},{56,48},{64,56},{72,6... | collective-permute-start | bytes 12296 | tf_op jit(solution)/shard_map/ppermute | solution.py:29
  16.8 2.1 %copy-start.12 = (s32[1,2,48]{2,1,0:T(2,128)S(1)}, s32[1,2,48]{2,1,0:T(2,128)}, u32[]{:S(2)}) copy-start(s32[1,2,48]{2,1,0:T(2,128)} %param.66) | copy-start | bytes 1156
  16.8 2.3 %copy-start.10 = (s32[1,4,8]{2,1,0:T(4,128)S(1)}, s32[1,4,8]{2,1,0:T(4,128)}, u32[]{:S(2)}) copy-start(s32[1,4,8]{2,1,0:T(4,128)} %param.67) | copy-start | bytes 388
  16.9 2.4 %copy-start.6 = (s32[1,2,1024]{2,1,0:T(2,128)S(1)}, s32[1,2,1024]{2,1,0:T(2,128)}, u32[]{:S(2)}) copy-start(s32[1,2,1024]{2,1,0:T(2,128)} %param.65) | copy-start | bytes 24580
  16.9 44.6 %collective-permute-start = (f32[2,2,2,128]{3,2,1,0:T(2,128)S(1)}, f32[2,2,2,128]{3,2,1,0:T(2,128)S(1)}, u32[]{:S(2)}, u32[]{:S(2)}) collective-permute-start(f32[2,2,2,128]{3,2,1,0:T(2,128)S(1)} %get-tuple-element.361), channel_id=1, source_target_pairs={{0,8},{8,16},{16,24},{24,32},{32,40},{40,48},{48,56},{56,64},{64,7... | collective-permute-start | bytes 12296 | tf_op jit(solution)/shard_map/ppermute | solution.py:26
  34.2 0.8 copy-start
  35.1 13.2 %copy-start.2 = (f32[8,2,8,128]{3,2,1,0:T(8,128)S(1)}, f32[8,2,8,128]{3,2,1,0:T(8,128)}, u32[]{:S(2)}) copy-start(f32[8,2,8,128]{3,2,1,0:T(8,128)} %param.61) | copy-start | bytes 196612
  60.8 0.7 copy-start.7
  60.8 0.7 copy-start.8
  61.5 7.4 %copy-start.1 = (f32[8,2,8,128]{3,2,1,0:T(8,128)S(1)}, f32[8,2,8,128]{3,2,1,0:T(8,128)}, u32[]{:S(2)}) copy-start(f32[8,2,8,128]{3,2,1,0:T(8,128)} %param.62) | copy-start | bytes 196612
  61.6 23.3 %collective-permute-start.2 = (f32[2,2,12,2]{3,2,1,0:T(8,128)S(1)}, f32[2,2,12,2]{3,2,1,0:T(8,128)S(1)}, u32[]{:S(2)}, u32[]{:S(2)}) collective-permute-start(f32[2,2,12,2]{3,2,1,0:T(8,128)S(1)} %get-tuple-element.360), channel_id=1, source_target_pairs={{0,1},{1,2},{2,3},{3,4},{4,5},{5,6},{6,7},{7,0},{8,9},{9,10},{10,1... | collective-permute-start | bytes 1160 | tf_op jit(solution)/shard_map/ppermute | solution.py:26
  67.0 17.9 %collective-permute-start.3 = (f32[2,2,12,2]{3,2,1,0:T(8,128)S(1)}, f32[2,2,12,2]{3,2,1,0:T(8,128)S(1)}, u32[]{:S(2)}, u32[]{:S(2)}) collective-permute-start(f32[2,2,12,2]{3,2,1,0:T(8,128)S(1)} %get-tuple-element.359), channel_id=1, source_target_pairs={{1,0},{2,1},{3,2},{4,3},{5,4},{6,5},{7,6},{0,7},{9,8},{10,9},{11,1... | collective-permute-start | bytes 1160 | tf_op jit(solution)/shard_map/ppermute | solution.py:29
  85.3 0.8 copy-start.4
  86.2 0.8 copy-start.5
  97.5 2.6 %copy-start.9 = (s32[8,2,8,128]{3,2,1,0:T(8,128)S(1)}, s32[8,2,8,128]{3,2,1,0:T(8,128)}, u32[]{:S(2)}) copy-start(s32[8,2,8,128]{3,2,1,0:T(8,128)} %param.64) | copy-start | bytes 196612
  113.3 13.7 %copy-start.3 = (f32[8,2,8,128]{3,2,1,0:T(8,128)}, f32[8,2,8,128]{3,2,1,0:T(8,128)S(1)}, u32[]{:S(2)}) copy-start(f32[8,2,8,128]{3,2,1,0:T(8,128)S(1)} %constant_dynamic-update-slice_fusion) | copy-start | bytes 196612
  128.1 29.1 %collective-permute-start.4 = (f32[2,1,130]{2,1,0:T(1,128)S(1)}, f32[2,1,130]{2,1,0:T(1,128)S(1)}, u32[]{:S(2)}, u32[]{:S(2)}) collective-permute-start(f32[2,1,130]{2,1,0:T(1,128)S(1)} %get-tuple-element.349), channel_id=1, source_target_pairs={{0,8},{8,16},{16,24},{24,32},{32,40},{40,48},{48,56},{56,64},{64,7... | collective-permute-start | bytes 3128 | tf_op jit(solution)/shard_map/ppermute | solution.py:26
  130.0 27.2 %collective-permute-start.5 = (f32[2,1,130]{2,1,0:T(1,128)S(1)}, f32[2,1,130]{2,1,0:T(1,128)S(1)}, u32[]{:S(2)}, u32[]{:S(2)}) collective-permute-start(f32[2,1,130]{2,1,0:T(1,128)S(1)} %get-tuple-element.348), channel_id=1, source_target_pairs={{8,0},{16,8},{24,16},{32,24},{40,32},{48,40},{56,48},{64,56},{72,6... | collective-permute-start | bytes 3128 | tf_op jit(solution)/shard_map/ppermute | solution.py:29
  143.2 31.3 %collective-permute-start.8 = (f32[6,1,1040]{2,0,1:T(8,128)S(1)}, f32[6,1,1040]{2,0,1:T(8,128)S(1)}, u32[]{:S(2)}, u32[]{:S(2)}) collective-permute-start(f32[6,1,1040]{2,0,1:T(8,128)S(1)} %bitcast.127), channel_id=1, source_target_pairs={{0,8},{8,16},{16,24},{24,32},{32,40},{40,48},{48,56},{56,64},{64,7... | collective-permute-start | bytes 74888 | tf_op jit(solution)/shard_map/ppermute | solution.py:26
  145.2 29.2 %collective-permute-start.9 = (f32[6,1,1040]{2,0,1:T(8,128)S(1)}, f32[6,1,1040]{2,0,1:T(8,128)S(1)}, u32[]{:S(2)}, u32[]{:S(2)}) collective-permute-start(f32[6,1,1040]{2,0,1:T(8,128)S(1)} %bitcast.128), channel_id=1, source_target_pairs={{8,0},{16,8},{24,16},{32,24},{40,32},{48,40},{56,48},{64,56},{72,6... | collective-permute-start | bytes 74888 | tf_op jit(solution)/shard_map/ppermute | solution.py:29
  157.3 8.4 %collective-permute-start.6 = (f32[2,12,1]{2,1,0:T(8,128)S(1)}, f32[2,12,1]{2,1,0:T(8,128)S(1)}, u32[]{:S(2)}, u32[]{:S(2)}) collective-permute-start(f32[2,12,1]{2,1,0:T(8,128)S(1)} %get-tuple-element.347), channel_id=1, source_target_pairs={{0,1},{1,2},{2,3},{3,4},{4,5},{5,6},{6,7},{7,0},{8,9},{9,10},{10,1... | collective-permute-start | bytes 296 | tf_op jit(solution)/shard_map/ppermute | solution.py:26
  163.6 6.9 %collective-permute-start.7 = (f32[2,12,1]{2,1,0:T(8,128)S(1)}, f32[2,12,1]{2,1,0:T(8,128)S(1)}, u32[]{:S(2)}, u32[]{:S(2)}) collective-permute-start(f32[2,12,1]{2,1,0:T(8,128)S(1)} %get-tuple-element.346), channel_id=1, source_target_pairs={{1,0},{2,1},{3,2},{4,3},{5,4},{6,5},{7,6},{0,7},{9,8},{10,9},{11,1... | collective-permute-start | bytes 296 | tf_op jit(solution)/shard_map/ppermute | solution.py:29
  174.7 5.1 %collective-permute-start.10 = (f32[6,1,64]{2,0,1:T(8,128)S(1)}, f32[6,1,64]{2,0,1:T(8,128)S(1)}, u32[]{:S(2)}, u32[]{:S(2)}) collective-permute-start(f32[6,1,64]{2,0,1:T(8,128)S(1)} %maximum_bitcast_fusion), channel_id=1, source_target_pairs={{0,1},{1,2},{2,3},{3,4},{4,5},{5,6},{6,7},{7,0},{8,9},{9,10},{10,1... | collective-permute-start | bytes 4616 | tf_op jit(solution)/shard_map/ppermute | solution.py:26
  176.7 6.7 %collective-permute-start.11 = (f32[6,1,64]{2,0,1:T(8,128)S(1)}, f32[6,1,64]{2,0,1:T(8,128)S(1)}, u32[]{:S(2)}, u32[]{:S(2)}) collective-permute-start(f32[6,1,64]{2,0,1:T(8,128)S(1)} %maximum_bitcast_fusion.1), channel_id=1, source_target_pairs={{1,0},{2,1},{3,2},{4,3},{5,4},{6,5},{7,6},{0,7},{9,8},{10,9},{11,1... | collective-permute-start | bytes 4616 | tf_op jit(solution)/shard_map/ppermute | solution.py:29
  (5 other events, 3.3 us)
where the time goes:
time: 186 us; the launch traced here: 185 us
  local copies, waits for them, and re-layouts  98.6 us (53%)
  starting transfers between devices  64.3 us (35%)
  other arithmetic  12.1 us (7%)
  waiting for transfers between devices  8.21 us (4%)
    gather x15, local copies, waits for them, and re-layouts, make_records(): jnp.take(single, flat_index).reshape(list_rows, list_length)  68.1 us
    ppermute x6, starting transfers between devices, with_halo(): lax.ppermute(lax.slice_in_dim(block, 0, width, axis=dim), axis, backward)  44.9 us
    ppermute x6, starting transfers between devices, with_halo(): lax.ppermute(lax.slice_in_dim(block, block.shape[dim] - width, None, axis...  19.5 us
    scatter x1, local copies, waits for them, and re-layouts, per_device(): departed = jnp.zeros((slot_count,), jnp.float32).at[jnp.where(all_lists >...  11.2 us
    scatter-add x9, local copies, waits for them, and re-layouts, per_device(): source_ext = source_ext.at[:, shift_x:shift_x + cells_x, shift_y:shift_y...  9.08 us
    ppermute x6, waiting for transfers between devices, with_halo(): lax.ppermute(lax.slice_in_dim(block, 0, width, axis=dim), axis, backward)  8.19 us
    another operation x6, other arithmetic  5.29 us
    unnamed x50, local copies, waits for them, and re-layouts  4.12 us
  transfers between devices with their start and end apart: 12, of which 2 were waited for; matrix products, arithmetic and copies ran while one was open for 34% of the time, Pallas kernels for 0%

commit v1 on v0

v1 whole, which is shorter than its diff:
```python
import jax
import jax.numpy as jnp
from jax import lax
from jax.experimental import pallas as pl
from jax.experimental.pallas import tpu as pltpu
from jax.sharding import PartitionSpec as P


NEWTON = 4
MIX_HORIZONTAL = 0.2
MIX_VERTICAL = 0.05
EXCESS_FACTOR = 4.2222
CURVATURE = 0.0012
KAPPA_SOLUTE = 0.6
GROWTH_STEP = 200.0
COLLIDE_RATE = 4e-07
VAPOUR_PER_SOURCE = 0.001
WARMING_FACTOR = 0.00249

F32 = jnp.float32
I32 = jnp.int32
SD = 8
FIELDS = 6

G_AIR = 0
G_DROP = 32
G_LIST = 80
G_ROWS = 88
X_DROP = 0
X_AIR = 96
X_EXT = 128
X_CORNER = 160
X_LIST = 208
X_SMALL = 216
X_ROWS = 224


def lanes_of(shape):
    return lax.broadcasted_iota(I32, shape, len(shape) - 1)


def rows_of(shape):
    return lax.broadcasted_iota(I32, shape, len(shape) - 2)


def pack_gy_kernel(q_ref, t_ref, sz_ref, wt_ref, dn_ref, ox_ref, oy_ref, pm_ref, small_ref, g_ref):
    g_ref[G_AIR : G_AIR + 16, :] = q_ref[...]
    g_ref[G_AIR + 16 : G_AIR + 32, :] = t_ref[...]
    lane = lanes_of((8, 128))
    first = lane < 32
    low_level = lane % 32 < 16
    for f, ref in enumerate((sz_ref, wt_ref, dn_ref, ox_ref, oy_ref, pm_ref)):
        parts = [ref[k * 16 : k * 16 + 16, :] for k in range(SD - 1, -1, -1)]
        block = jnp.concatenate(parts, 0)
        if f == 5:
            block = block.astype(F32)
        turned = jnp.transpose(block)
        sides = []
        for row in (127, 0):
            line = jnp.broadcast_to(turned[row : row + 1, :], (8, 128))
            sides.append(line)
        out = []
        for n, line in enumerate(sides):
            base = 32 * n
            line = pltpu.roll(line, 16, 1, stride=16, stride_axis=0)
            lev0 = pltpu.roll(line, base + 4, 1)
            lev1 = pltpu.roll(line, base + 12, 1)
            out.append(jnp.where(low_level, lev0, lev1))
        g_ref[G_DROP + f * 8 : G_DROP + f * 8 + 8, :] = jnp.where(first, out[0], out[1])
    g_ref[G_LIST : G_LIST + 8, :] = jnp.broadcast_to(small_ref[...], (8, 128))


def pack_gx_kernel(
    q_ref, t_ref, sz_ref, wt_ref, dn_ref, ox_ref, oy_ref, pm_ref, list_ref, south_ref, north_ref,
    east_ref, west_ref,
):
    lane16 = lanes_of((16, 128))
    ext = []
    for a in range(2):
        rows = slice(G_AIR + 16 * a, G_AIR + 16 * a + 16)
        ext.append(jnp.where(lane16 < 64, north_ref[rows, :], south_ref[rows, :]))
    lane = lanes_of((8, 128))
    small = jnp.where(
        (lane < 48) | ((lane >= 96) & (lane < 112)),
        south_ref[G_LIST : G_LIST + 8, :],
        north_ref[G_LIST : G_LIST + 8, :],
    )
    corners = []
    for f in range(FIELDS):
        rows = slice(G_DROP + 8 * f, G_DROP + 8 * f + 8)
        corners.append(jnp.where(lane < 32, south_ref[rows, :], north_ref[rows, :]))
    refs = (sz_ref, wt_ref, dn_ref, ox_ref, oy_ref, pm_ref)
    for side, (out_ref, i) in enumerate(((east_ref, 7), (west_ref, 0))):
        for f, ref in enumerate(refs):
            face = ref[pl.ds(i, 16, stride=8), :]
            if f == 5:
                face = face.astype(F32)
            out_ref[X_DROP + 16 * f : X_DROP + 16 * f + 16, :] = face
            out_ref[X_CORNER + 8 * f : X_CORNER + 8 * f + 8, :] = corners[f]
        out_ref[X_AIR : X_AIR + 16, :] = q_ref[...]
        out_ref[X_AIR + 16 : X_AIR + 32, :] = t_ref[...]
        out_ref[X_EXT : X_EXT + 16, :] = ext[0]
        out_ref[X_EXT + 16 : X_EXT + 32, :] = ext[1]
        out_ref[X_LIST : X_LIST + 8, :] = list_ref[side].astype(F32)
        out_ref[X_SMALL : X_SMALL + 8, :] = small


def departed_kernel(list_ref, small_ref, mask_ref):
    entries = jnp.concatenate(
        [list_ref[0, r : r + 1, :] for r in range(8)]
        + [list_ref[1, r : r + 1, :] for r in range(8)]
        + [small_ref[...].astype(I32)],
        1,
    )
    width = entries.shape[1]
    index = rows_of((128, width))
    row = jnp.broadcast_to(entries >> 7, (128, width))
    column = jnp.broadcast_to(entries & 127, (128, width))
    one_row = jnp.where(row == index, 1.0, 0.0).astype(jnp.bfloat16)
    one_column = jnp.where(column == index, 1.0, 0.0).astype(jnp.bfloat16)
    mask_ref[...] = lax.dot_general(
        one_row, one_column, (((1,), (1,)), ((), ())), preferred_element_type=F32
    )


def kernel_weights(offset):
    return (
        jnp.maximum(0.5 - offset, 0.0),
        1.0 - jnp.abs(offset - 0.5),
        jnp.maximum(offset - 0.5, 0.0),
    )


def cube_root(x):
    y = jnp.exp(jnp.log(x) * (1.0 / 3.0))
    return y - (y * y * y - x) / (3.0 * y * y)


def grow(size, dry, forcing):
    initial = size * size
    lowest = dry * dry
    solute = KAPPA_SOLUTE * lowest * dry
    wetted = initial
    for _ in range(NEWTON):
        root = lax.rsqrt(wetted)
        inverse_square = root * root
        inverse = inverse_square * root
        residue = wetted - initial - GROWTH_STEP * (forcing + solute * inverse)
        slope = 1.0 + (1.5 * GROWTH_STEP) * solute * (inverse * inverse_square)
        wetted = jnp.maximum(wetted - residue / slope, lowest)
    return wetted


def pick(values, bits):
    low, mid, high = bits
    a = [jnp.where(low, values[2 * n + 1], values[2 * n]) for n in range(4)]
    b = [jnp.where(mid, a[2 * n + 1], a[2 * n]) for n in range(2)]
    return jnp.where(high, b[1], b[0])


def coalesce(grown, mult, order):
    bits = [((o & 1) == 1, (o & 2) == 2, (o & 4) == 4) for o in order]
    new_radius, new_mult = [], []
    for pair in range(SD // 2):
        p, q = bits[2 * pair], bits[2 * pair + 1]
        r1, r2 = pick(grown, p), pick(grown, q)
        m1, m2 = pick(mult, p), pick(mult, q)
        big = m1 >= m2
        hr, lr = jnp.where(big, r1, r2), jnp.where(big, r2, r1)
        hm, lm = jnp.where(big, m1, m2), jnp.where(big, m2, m1)
        total = r1 + r2
        rate = COLLIDE_RATE * hm * total * total * jnp.abs(r1 * r1 - r2 * r2)
        chance = 1.0 - jnp.exp(-rate)
        merged = cube_root(lr * lr * lr + chance * hr * hr * hr)
        reduced = hm - chance * lm
        new_radius += [jnp.where(big, hr, merged), jnp.where(big, merged, hr)]
        new_mult += [jnp.where(big, reduced, lm), jnp.where(big, lm, reduced)]
    out_radius, out_mult = [], []
    for target in range(SD):
        r, m = new_radius[0], new_mult[0]
        for position in range(1, SD):
            hit = order[position] == target
            r = jnp.where(hit, new_radius[position], r)
            m = jnp.where(hit, new_mult[position], m)
        out_radius.append(r)
        out_mult.append(m)
    return out_radius, out_mult


def shift(x, amount, axis):
    return pltpu.roll(x, amount % x.shape[axis], axis)


def droplets(windows, size, mult, dry, east, north, order):
    deposit = [[None] * 3 for _ in range(3)]
    grown = []
    for k in range(SD):
        wx, wy = kernel_weights(east[k]), kernel_weights(north[k])
        forcing = -(CURVATURE / size[k])
        for a in range(3):
            line = wy[0] * windows[a][0] + wy[1] * windows[a][1] + wy[2] * windows[a][2]
            forcing = forcing + wx[a] * line
        wetted = grow(size[k], dry[k], forcing)
        radius = jnp.sqrt(wetted)
        condensed = mult[k] * (wetted * radius - size[k] * size[k] * size[k])
        for a in range(3):
            part = wx[a] * condensed
            for b in range(3):
                term = part * wy[b]
                deposit[a][b] = term if k == 0 else deposit[a][b] + term
        grown.append(radius)
    radius, coalesced = coalesce(grown, mult, order)
    return radius, coalesced, deposit


def physics_kernel(
    q_ref, t_ref, sz_ref, wt_ref, dn_ref, ox_ref, oy_ref, pm_ref, mask_ref,
    south_ref, north_ref, west_ref, east_ref,
    moist_ref, warm_ref, size_ref, mult_ref, record_ref, box_ref,
    halo_ref, table_ref,
):
    lane16 = lanes_of((16, 128))
    lane = lanes_of((8, 128))
    row8 = rows_of((8, 128))
    slot = lane % 16

    air = []
    for a, own_ref in enumerate((q_ref, t_ref)):
        g_rows = slice(G_AIR + 16 * a, G_AIR + 16 * a + 16)
        ext = jnp.where(lane16 < 64, north_ref[g_rows, :], south_ref[g_rows, :])
        levels = []
        for l in range(2):
            rows = []
            for ref in (west_ref, None, east_ref):
                if ref is None:
                    main = own_ref[8 * l : 8 * l + 8, :]
                    side = ext[8 * l : 8 * l + 8, :]
                else:
                    base = 16 * a + 8 * l
                    main = ref[X_AIR + base : X_AIR + base + 8, :]
                    side = ref[X_EXT + base : X_EXT + base + 8, :]
                rows.append(jnp.concatenate([main, side], 1))
            levels.append(jnp.concatenate(rows, 0))
        air.append(levels)
    mixed = []
    for a in range(2):
        both = []
        for l in range(2):
            x = air[a][l]
            other = air[a][1 - l]
            across = (
                shift(x, 1, 0) + shift(x, -1, 0) + shift(x, 1, 1) + shift(x, -1, 1) - 4.0 * x
            )
            both.append(x + MIX_HORIZONTAL * across + MIX_VERTICAL * (other + x - 2.0 * x))
        mixed.append(both)
    moved = []
    turned = []
    for l in range(2):
        vapour, warm = mixed[0][l], mixed[1][l]
        most = EXCESS_FACTOR * jnp.exp(17.27 * (warm - 273.15) / (warm - 35.86))
        humid = vapour / most - 1.0
        columns = [shift(humid, 1, 1), humid, shift(humid, -1, 1)]
        moved.append([[shift(c[:, :128], 1, 0) for c in columns],
                      [c[:, :128] for c in columns],
                      [shift(c[:, :128], -1, 0) for c in columns]])
        ahead = shift(humid, 2, 1)
        tall = lanes_of((24, 128))
        near = jnp.where(tall < 8, ahead[:, :128], shift(ahead[:, 128:], 8, 1))
        turned.append(near[4:20, :])
    strip = jnp.concatenate(turned + turned + turned + turned, 0)
    strip = jnp.transpose(strip)
    lane1 = lanes_of((1, 128))
    rim = []
    for b in range(3):
        line = jnp.where(lane1 < 32, strip[b : b + 1, :], strip[b + 9 : b + 10, :])
        rim.append([shift(line, 1, 1), line, shift(line, -1, 1)])

    beyond = []
    for f in range(FIELDS):
        c_rows = slice(X_CORNER + 8 * f, X_CORNER + 8 * f + 8)
        g_rows = slice(G_DROP + 8 * f, G_DROP + 8 * f + 8)
        own = jnp.where(lane < 32, south_ref[g_rows, :], north_ref[g_rows, :])
        line = jnp.where(
            slot == 3,
            shift(west_ref[c_rows, :], -8, 1),
            jnp.where(slot == 12, shift(east_ref[c_rows, :], 8, 1), own),
        )
        line = jnp.where((lane < 64) & (slot >= 3) & (slot <= 12), line, 0.0 if f == 5 else 0.5)
        beyond.append(line)
        for l in range(2):
            base = X_DROP + 16 * f + l
            halo_ref[f, pl.ds(l, 8, stride=8), :] = west_ref[pl.ds(base, 8, stride=2), :]
            halo_ref[f, pl.ds(2 + l, 8, stride=8), :] = east_ref[pl.ds(base, 8, stride=2), :]
        for r in range(4, 8):
            halo_ref[f, pl.ds(r, 8, stride=8), :] = line

    deposits = []
    for l in range(2):
        windows = [[moved[l][a][b][8:16, :] for b in range(3)] for a in range(3)]
        tiles = [
            [ref[k * 16 + 8 * l : k * 16 + 8 * l + 8, :] for k in range(SD)]
            for ref in (sz_ref, wt_ref, dn_ref, ox_ref, oy_ref, pm_ref)
        ]
        radius, coalesced, deposit = droplets(windows, *tiles)
        for k in range(SD):
            rows = slice(k * 16 + 8 * l, k * 16 + 8 * l + 8)
            size_ref[rows, :] = radius[k]
            mult_ref[rows, :] = jnp.where(mask_ref[rows, :] > 0.5, 0.0, coalesced[k])
        deposits.append(deposit)
    windows = []
    for a in range(3):
        line = []
        for b in range(3):
            line.append(jnp.concatenate(
                [moved[0][a][b][7:8, :], moved[1][a][b][7:8, :],
                 moved[0][a][b][16:17, :], moved[1][a][b][16:17, :]] + [rim[b][a]] * 4, 0))
        windows.append(line)
    tiles = [[halo_ref[f, 8 * k : 8 * k + 8, :] for k in range(SD)] for f in range(5)]
    order = [halo_ref[5, 8 * k : 8 * k + 8, :].astype(I32) for k in range(SD)]
    halo_radius, halo_mult, outer = droplets(windows, *tiles, order)
    for k in range(SD):
        table_ref[0, 8 * k : 8 * k + 8, :] = halo_radius[k]
        table_ref[1, 8 * k : 8 * k + 8, :] = halo_mult[k]

    def along_y(d, a):
        return (
            d[a][1]
            + jnp.where(lane == 0, 0.0, shift(d[a][2], 1, 1))
            + jnp.where(lane == 127, 0.0, shift(d[a][0], -1, 1))
        )

    from_west = along_y(outer, 2)
    from_east = along_y(outer, 0)
    rim_line = [jnp.where(lane1 < 32, outer[a][2][4:5, :], outer[a][0][4:5, :]) for a in range(3)]
    rim_line = shift(rim_line[2], 1, 1) + rim_line[1] + shift(rim_line[0], -1, 1)
    rim_line = jnp.broadcast_to(rim_line, (8, 128))
    for l in range(2):
        own = [along_y(deposits[l], a) for a in range(3)]
        west_row = jnp.broadcast_to(from_west[l : l + 1, :], (8, 128))
        east_row = jnp.broadcast_to(from_east[2 + l : 3 + l, :], (8, 128))
        source = (
            own[1]
            + jnp.where(row8 == 0, west_row, shift(own[2], 1, 0))
            + jnp.where(row8 == 7, east_row, shift(own[0], -1, 0))
        )
        for side, j in enumerate((0, 127)):
            wanted = lane == side * 32 + l * 16 + 4 + row8
            column = jnp.sum(jnp.where(wanted, rim_line, 0.0), axis=1, keepdims=True)
            source = source + jnp.where(lane == j, column, 0.0)
        rows = slice(8 * l, 8 * l + 8)
        moist_ref[rows, :] = mixed[0][l][8:16, :128] - VAPOUR_PER_SOURCE * source
        warm_ref[rows, :] = mixed[1][l][8:16, :128] + WARMING_FACTOR * source

    for side, (ref, dx) in enumerate(((west_ref, 1), (east_ref, -1))):
        entry = ref[X_LIST : X_LIST + 8, :].astype(I32)
        live = entry >= 0
        column = entry & 127
        group = entry >> 10
        picked = [jnp.zeros((8, 128), F32) for _ in range(5)]
        for k in range(SD):
            for l in range(2):
                here = live & (group == 2 * k + l)
                r = 8 * k + 2 * side + l
                for n in range(5):
                    src = table_ref if n < 2 else halo_ref
                    line = jnp.broadcast_to(src[n, r : r + 1, :], (8, 128))
                    got = jnp.take_along_axis(line, column, axis=1)
                    picked[n] = jnp.where(here, got, picked[n])
        box = (((entry >> 10) & 1) * 8 + (((entry >> 7) + dx) & 7)) * 128 + column
        box = jnp.where(live, box, -1)
        for c in range(8):
            at = side * 1024 + c * 128
            for n in range(5):
                record_ref[n, 0:1, at : at + 128] = picked[n][c : c + 1, :]
            box_ref[0:1, at : at + 128] = box[c : c + 1, :]

    own_small = jnp.where(
        (lane < 48) | ((lane >= 96) & (lane < 112)),
        south_ref[G_LIST : G_LIST + 8, :],
        north_ref[G_LIST : G_LIST + 8, :],
    )
    diagonal = lane >= 96
    by_west = diagonal & (lane % 16 < 8)
    entry = jnp.where(
        by_west,
        west_ref[X_SMALL : X_SMALL + 8, :],
        jnp.where(diagonal, east_ref[X_SMALL : X_SMALL + 8, :], own_small),
    ).astype(I32)
    live = entry >= 0
    north_side = ((lane >= 48) & (lane < 96)) | (lane >= 112)
    column = entry & 127
    i = (entry >> 7) & 7
    level = (entry >> 10) & 1
    place = i + 4 + jnp.where(diagonal, jnp.where(by_west, -8, 8), 0)
    at = (jnp.where(north_side, 32, 0) + level * 16 + place) & 127
    mine = live & ((entry >> 11) == row8)
    dx = jnp.where(diagonal, jnp.where(by_west, 1, -1), 0)
    dy = jnp.where(north_side, -1, 1)
    box = (level * 8 + ((i + dx) & 7)) * 128 + ((column + dy) & 127)
    box_ref[0:1, 2048:2176] = jnp.where(live, box, -1)[0:1, :]
    for n in range(5):
        if n < 2:
            table = table_ref[n, pl.ds(4, 8, stride=8), :]
        else:
            table = beyond[n]
        got = jnp.take_along_axis(table, at, axis=1)
        line = jnp.sum(jnp.where(mine, got, 0.0), axis=0, keepdims=True)
        record_ref[n, 0:1, 2048:2176] = line


def whole(count):
    return [pl.BlockSpec(memory_space=pltpu.VMEM)] * count


def call(kernel, outs, args, scratch=(), flops=1 << 20):
    return pl.pallas_call(
        kernel,
        out_shape=outs,
        in_specs=whole(len(args)),
        out_specs=jax.tree.map(lambda _: pl.BlockSpec(memory_space=pltpu.VMEM), outs),
        scratch_shapes=list(scratch),
        cost_estimate=pl.CostEstimate(flops=flops, bytes_accessed=1 << 18, transcendentals=0),
    )(*args)


def ring(axis, step):
    count = lax.axis_size(axis)
    return [(i, (i + step) % count) for i in range(count)]


def per_device(
    moisture_ratio,
    kelvin_warmth,
    droplet_size_micron,
    weighting_factor,
    dry_nucleus_size,
    fractional_offset_east,
    fractional_offset_north,
    encounter_permutation,
    departing_eastwest_lists,
    departing_northsouth_lists,
    departing_diagonal_lists,
):
    def f32(*shape):
        return jax.ShapeDtypeStruct(shape, F32)

    air = (moisture_ratio.reshape(16, 128), kelvin_warmth.reshape(16, 128))
    drops = tuple(
        x.reshape(128, 128)
        for x in (
            droplet_size_micron,
            weighting_factor,
            dry_nucleus_size,
            fractional_offset_east,
            fractional_offset_north,
            encounter_permutation,
        )
    )
    long_lists = departing_eastwest_lists.reshape(2, 8, 128)
    corner = departing_diagonal_lists[0]
    small = (
        jnp.concatenate(
            [departing_northsouth_lists.reshape(-1), corner[0], corner[2], corner[1], corner[3]]
        )
        .astype(F32)
        .reshape(1, 128)
    )
    to_gy = call(pack_gy_kernel, f32(G_ROWS, 128), (*air, *drops, small))
    from_south = lax.ppermute(to_gy, "gy", ring("gy", 1))
    from_north = lax.ppermute(to_gy, "gy", ring("gy", -1))
    to_east, to_west = call(
        pack_gx_kernel,
        (f32(X_ROWS, 128), f32(X_ROWS, 128)),
        (*air, *drops, long_lists, from_south, from_north),
    )
    from_west = lax.ppermute(to_east, "gx", ring("gx", 1))
    from_east = lax.ppermute(to_west, "gx", ring("gx", -1))
    departed = call(departed_kernel, f32(128, 128), (long_lists, small))
    moist, warm, size, mult, records, box = call(
        physics_kernel,
        (
            f32(16, 128),
            f32(16, 128),
            f32(128, 128),
            f32(128, 128),
            f32(5, 1, 2176),
            jax.ShapeDtypeStruct((1, 2176), I32),
        ),
        (*air, *drops, departed, from_south, from_north, from_west, from_east),
        scratch=(pltpu.VMEM((FIELDS, 64, 128), F32), pltpu.VMEM((2, 64, 128), F32)),
    )
    return (
        moist.reshape(moisture_ratio.shape),
        warm.reshape(kelvin_warmth.shape),
        size.reshape(droplet_size_micron.shape),
        mult.reshape(weighting_factor.shape),
        records,
        box,
    )


def solution(mesh):
    cells = P(None, "gx", "gy")
    drop = P(None, None, "gx", "gy")
    lists = P("gx", None, "gy")
    return jax.shard_map(
        per_device,
        mesh=mesh,
        in_specs=(cells,) * 2 + (drop,) * 6 + (lists,) * 3,
        out_specs=(cells, cells, drop, drop, P(None, "gx", "gy"), P("gx", "gy")),
        check_vma=False,
    )
```

time: 186 us -> 43.9 us (0.24)
  the two profiles are of different devices: /device:TPU:25 before, /device:TPU:8 now
where the time goes in v1:
time: 43.9 us; the launch traced here: 43.4 us
  starting transfers between devices  20.3 us (46%)
  waiting for transfers between devices  9.74 us (22%)
  Pallas kernels  8.61 us (20%)
  local copies, waits for them, and re-layouts  3.56 us (8%)
  between operations  0.68 us (2%)
  other arithmetic  0.52 us (1%)
    ppermute x1, starting transfers between devices, per_device(): from_east = lax.ppermute(to_west, 'gx', ring('gx', -1))  12.6 us
    pallas_call x4, Pallas kernels, call(): pl.pallas_call(kernel, out_shape=outs, in_specs=whole(len(args)), out_spe...  8.61 us
    ppermute x1, waiting for transfers between devices, per_device(): from_south = lax.ppermute(to_gy, 'gy', ring('gy', 1))  6.71 us
    ppermute x1, starting transfers between devices, per_device(): from_west = lax.ppermute(to_east, 'gx', ring('gx', 1))  3.43 us
    ppermute x1, starting transfers between devices, per_device(): from_south = lax.ppermute(to_gy, 'gy', ring('gy', 1))  2.41 us
    ppermute x1, starting transfers between devices, per_device(): from_north = lax.ppermute(to_gy, 'gy', ring('gy', -1))  1.91 us
    unnamed x11, local copies, waits for them, and re-layouts  1.87 us
    ppermute x1, waiting for transfers between devices, per_device(): from_west = lax.ppermute(to_east, 'gx', ring('gx', 1))  1.85 us
  transfers between devices with their start and end apart: 4, of which 3 were waited for; matrix products, arithmetic and copies ran while one was open for 1% of the time, Pallas kernels for 4%

profile of v1, /device:TPU:8, one launch (start us, length us, event | category | flops | bytes accessed | tf_op | source)
XLA Modules:
  0.0 43.4 jit_solution(14495438377218879956)
XLA Ops:
  0.6 0.8 %concatenate.20 = s32[1,96]{1,0:T(1,128)S(1)} reshape(s32[1,2,48]{2,1,0:T(2,128)} %param.20) | data formatting | bytes 768 | tf_op jit(solution)/shard_map/concatenate | solution.py:462
  1.4 0.8 %slice_bitcast_fusion = (s32[1,8]{1,0:T(1,128)S(1)}, s32[1,8]{1,0:T(1,128)S(1)}, s32[1,8]{1,0:T(1,128)S(1)}, s32[1,8]{1,0:T(1,128)S(1)}) fusion(s32[1,4,8]{2,1,0:T(4,128)} %param.21), kind=kLoop, calls=%fused_computation.1 | loop fusion | bytes 256 | tf_op jit(solution)/shard_map/concatenate | solution.py:462
  2.2 0.1 concatenate.25
  2.3 0.5 %convert_element_type.10.small_ref = f32[1,128]{1,0:T(1,128)} convert(s32[1,128]{1,0:T(1,128)S(1)} %concatenate.25) | non-fusion elementwise | flops 128 | bytes 1024 | tf_op jit(solution)/shard_map/convert_element_type | solution.py:465
  2.8 0.0 copy-start.4
  2.8 2.1 %shard_map.155 = f32[88,128]{1,0:T(8,128)} custom-call(f32[16,128]{1,0:T(8,128)} %bitcast.43, f32[16,128]{1,0:T(8,128)} %bitcast.46, f32[128,128]{1,0:T(8,128)} %bitcast.25, f32[128,128]{1,0:T(8,128)} %bitcast.28, f32[128,128]{1,0:T(8,128)} %bitcast.31, f32[128,128]{1,0:T(8,128)} %bitcast.34, f32[128,128]{1,0:T(8,128)} %bitcast.37, s32[128,128]{1,0:T(8,128)} %bitcast.40, ...), custom_call_target="tpu_custom_call" | custom-call | flops 1048576 | bytes 262144 | tf_op jit(solution)/shard_map/pallas_call | solution.py:416
  5.0 1.9 %collective-permute-start.1 = (f32[88,128]{1,0:T(8,128)}, f32[88,128]{1,0:T(8,128)S(1)}, u32[]{:S(2)}, u32[]{:S(2)}) collective-permute-start(f32[88,128]{1,0:T(8,128)} %shard_map.155), channel_id=1, source_target_pairs={{0,7},{1,0},{2,1},{3,2},{4,3},{5,4},{6,5},{7,6},{8,15},{9,8},{10,9... | collective-permute-start | bytes 135176 | tf_op jit(solution)/shard_map/ppermute | solution.py:470
  6.9 2.4 %collective-permute-start = (f32[88,128]{1,0:T(8,128)}, f32[88,128]{1,0:T(8,128)S(1)}, u32[]{:S(2)}, u32[]{:S(2)}) collective-permute-start(f32[88,128]{1,0:T(8,128)} %shard_map.155), channel_id=1, source_target_pairs={{0,1},{1,2},{2,3},{3,4},{4,5},{5,6},{6,7},{7,0},{8,9},{9,10},{10,1... | collective-permute-start | bytes 135176 | tf_op jit(solution)/shard_map/ppermute | solution.py:469
  9.3 0.0 copy-done.4
  9.3 0.6 %copy.19 = s32[1,2,8,128]{3,2,1,0:T(8,128)} copy(s32[1,2,8,128]{3,1,2,0:T(2,128)S(1)} %bitcast.51) | data formatting | bytes 16384
  9.9 0.0 collective-permute-done.1.north_ref
  9.9 0.0 copy-start
  9.9 6.7 %collective-permute-done.south_ref = f32[88,128]{1,0:T(8,128)S(1)} collective-permute-done((f32[88,128]{1,0:T(8,128)}, f32[88,128]{1,0:T(8,128)S(1)}, u32[]{:S(2)}, u32[]{:S(2)}) %collective-permute-start) | collective-permute-done | bytes 45088 | tf_op jit(solution)/shard_map/ppermute | solution.py:469
  16.6 0.0 copy-done
  16.6 0.6 %copy-done.1 = f32[88,128]{1,0:T(8,128)} copy-done((f32[88,128]{1,0:T(8,128)}, f32[88,128]{1,0:T(8,128)S(1)}, u32[]{:S(2)}) %copy-start.1) | copy-done | bytes 45080
  17.2 1.8 %shard_map.156 = (f32[224,128]{1,0:T(8,128)}, f32[224,128]{1,0:T(8,128)}) custom-call(f32[16,128]{1,0:T(8,128)} %bitcast.44, f32[16,128]{1,0:T(8,128)} %bitcast.47, f32[128,128]{1,0:T(8,128)} %bitcast.26, f32[128,128]{1,0:T(8,128)} %bitcast.29, f32[128,128]{1,0:T(8,128)} %bitcast.32, f32[128,128]{1,0:T(8,128)} %bitcast.35, f32[128,128]{1,0:T(8,128)} %bitcast.38, ...), custom_call_target="tpu_custom_call" | custom-call | flops 1048576 | bytes 262144 | tf_op jit(solution)/shard_map/pallas_call | solution.py:416
  19.0 3.4 %collective-permute-start.2 = (f32[224,128]{1,0:T(8,128)}, f32[224,128]{1,0:T(8,128)S(1)}, u32[]{:S(2)}, u32[]{:S(2)}) collective-permute-start(f32[224,128]{1,0:T(8,128)} %get-tuple-element.14), channel_id=1, source_target_pairs={{0,8},{8,16},{16,24},{24,32},{32,40},{40,48},{48,56},{56,64},{64,7... | collective-permute-start | bytes 344072 | tf_op jit(solution)/shard_map/ppermute | solution.py:476
  22.4 12.6 %collective-permute-start.3 = (f32[224,128]{1,0:T(8,128)}, f32[224,128]{1,0:T(8,128)S(1)}, u32[]{:S(2)}, u32[]{:S(2)}) collective-permute-start(f32[224,128]{1,0:T(8,128)} %get-tuple-element.15), channel_id=1, source_target_pairs={{0,504},{8,0},{16,8},{24,16},{32,24},{40,32},{48,40},{56,48},{64,5... | collective-permute-start | bytes 344072 | tf_op jit(solution)/shard_map/ppermute | solution.py:477
  35.0 1.6 %shard_map.154.mask_ref = f32[128,128]{1,0:T(8,128)} custom-call(s32[2,8,128]{2,1,0:T(8,128)} %bitcast.50, f32[1,128]{1,0:T(1,128)} %convert_element_type.10.small_ref), custom_call_target="tpu_custom_call" | custom-call | flops 1048576 | bytes 262144 | tf_op jit(solution)/shard_map/pallas_call | solution.py:416
  36.7 1.8 %collective-permute-done.2.west_ref = f32[224,128]{1,0:T(8,128)S(1)} collective-permute-done((f32[224,128]{1,0:T(8,128)}, f32[224,128]{1,0:T(8,128)S(1)}, u32[]{:S(2)}, u32[]{:S(2)}) %collective-permute-start.2) | collective-permute-done | bytes 114720 | tf_op jit(solution)/shard_map/ppermute | solution.py:476
  38.5 1.2 %collective-permute-done.3.east_ref = f32[224,128]{1,0:T(8,128)S(1)} collective-permute-done((f32[224,128]{1,0:T(8,128)}, f32[224,128]{1,0:T(8,128)S(1)}, u32[]{:S(2)}, u32[]{:S(2)}) %collective-permute-start.3) | collective-permute-done | bytes 114720 | tf_op jit(solution)/shard_map/ppermute | solution.py:477
  39.7 0.0 copy-done.2
  39.7 0.7 %copy-done.3 = f32[224,128]{1,0:T(8,128)} copy-done((f32[224,128]{1,0:T(8,128)}, f32[224,128]{1,0:T(8,128)S(1)}, u32[]{:S(2)}) %copy-start.3) | copy-done | bytes 114712
  40.4 3.1 %shard_map.157 = (f32[16,128]{1,0:T(8,128)}, f32[16,128]{1,0:T(8,128)}, f32[128,128]{1,0:T(8,128)}, f32[128,128]{1,0:T(8,128)}, f32[5,1,2176]{2,1,0:T(1,128)}, /*index=5*/s32[1,2176]{1,0:T(1,128)}) custom-call(f32[16,128]{1,0:T(8,128)} %bitcast.45, f32[16,128]{1,0:T(8,128)} %bitcast.48, f32[128,128]{1,0:T(8,128)} %bitcast.27, f32[128,128]{1,0:T(8,128)} %bitcast.30, ...), custom_call_target="tpu_custom_call" | custom-call | flops 1048576 | bytes 262144 | tf_op jit(solution)/shard_map/pallas_call | solution.py:416
  (3 shorter events, 0.0 us)
Async XLA Ops:
  2.8 6.5 %copy-start.4 = (s32[1,2,1024]{2,1,0:T(2,128)S(1)}, s32[1,2,1024]{2,1,0:T(2,128)}, u32[]{:S(2)}) copy-start(s32[1,2,1024]{2,1,0:T(2,128)} %param.19) | copy-start | bytes 24580
  5.0 4.9 %collective-permute-start.1 = (f32[88,128]{1,0:T(8,128)}, f32[88,128]{1,0:T(8,128)S(1)}, u32[]{:S(2)}, u32[]{:S(2)}) collective-permute-start(f32[88,128]{1,0:T(8,128)} %shard_map.155), channel_id=1, source_target_pairs={{0,7},{1,0},{2,1},{3,2},{4,3},{5,4},{6,5},{7,6},{8,15},{9,8},{10,9... | collective-permute-start | bytes 135176 | tf_op jit(solution)/shard_map/ppermute | solution.py:470
  6.9 9.7 %collective-permute-start = (f32[88,128]{1,0:T(8,128)}, f32[88,128]{1,0:T(8,128)S(1)}, u32[]{:S(2)}, u32[]{:S(2)}) collective-permute-start(f32[88,128]{1,0:T(8,128)} %shard_map.155), channel_id=1, source_target_pairs={{0,1},{1,2},{2,3},{3,4},{4,5},{5,6},{6,7},{7,0},{8,9},{9,10},{10,1... | collective-permute-start | bytes 135176 | tf_op jit(solution)/shard_map/ppermute | solution.py:469
  9.9 6.7 %copy-start = (f32[88,128]{1,0:T(8,128)}, f32[88,128]{1,0:T(8,128)S(1)}, u32[]{:S(2)}) copy-start(f32[88,128]{1,0:T(8,128)S(1)} %collective-permute-done.1.north_ref) | copy-start | bytes 135172
  16.6 0.6 %copy-start.1 = (f32[88,128]{1,0:T(8,128)}, f32[88,128]{1,0:T(8,128)S(1)}, u32[]{:S(2)}) copy-start(f32[88,128]{1,0:T(8,128)S(1)} %collective-permute-done.south_ref) | copy-start | bytes 135172
  19.0 19.5 %collective-permute-start.2 = (f32[224,128]{1,0:T(8,128)}, f32[224,128]{1,0:T(8,128)S(1)}, u32[]{:S(2)}, u32[]{:S(2)}) collective-permute-start(f32[224,128]{1,0:T(8,128)} %get-tuple-element.14), channel_id=1, source_target_pairs={{0,8},{8,16},{16,24},{24,32},{32,40},{40,48},{48,56},{56,64},{64,7... | collective-permute-start | bytes 344072 | tf_op jit(solution)/shard_map/ppermute | solution.py:476
  22.4 17.3 %collective-permute-start.3 = (f32[224,128]{1,0:T(8,128)}, f32[224,128]{1,0:T(8,128)S(1)}, u32[]{:S(2)}, u32[]{:S(2)}) collective-permute-start(f32[224,128]{1,0:T(8,128)} %get-tuple-element.15), channel_id=1, source_target_pairs={{0,504},{8,0},{16,8},{24,16},{32,24},{40,32},{48,40},{56,48},{64,5... | collective-permute-start | bytes 344072 | tf_op jit(solution)/shard_map/ppermute | solution.py:477
  38.5 1.2 %copy-start.2 = (f32[224,128]{1,0:T(8,128)}, f32[224,128]{1,0:T(8,128)S(1)}, u32[]{:S(2)}) copy-start(f32[224,128]{1,0:T(8,128)S(1)} %collective-permute-done.2.west_ref) | copy-start | bytes 344068
  39.7 0.7 %copy-start.3 = (f32[224,128]{1,0:T(8,128)}, f32[224,128]{1,0:T(8,128)S(1)}, u32[]{:S(2)}) copy-start(f32[224,128]{1,0:T(8,128)S(1)} %collective-permute-done.3.east_ref) | copy-start | bytes 344068

commit v2 on v1

--- a/solution.py
+++ b/solution.py
@@ -22,105 +22,132 @@
 SD = 8
 FIELDS = 6
 
-G_AIR = 0
-G_DROP = 32
-G_LIST = 80
-G_ROWS = 88
-X_DROP = 0
-X_AIR = 96
-X_EXT = 128
-X_CORNER = 160
-X_LIST = 208
-X_SMALL = 216
-X_ROWS = 224
+G_LIST = 8 * FIELDS
+G_ROWS = G_LIST + 8
+X_AIR = 16 * FIELDS
+X_CORNER = X_AIR + 16
+X_LIST = X_CORNER + 8
+X_ROWS = X_LIST + 8
 
 
 def lanes_of(shape):
     return lax.broadcasted_iota(I32, shape, len(shape) - 1)
 
 
+def shift(x, amount, axis):
+    return pltpu.roll(x, amount % x.shape[axis], axis)
+
+
 def rows_of(shape):
     return lax.broadcasted_iota(I32, shape, len(shape) - 2)
 
 
-def pack_gy_kernel(q_ref, t_ref, sz_ref, wt_ref, dn_ref, ox_ref, oy_ref, pm_ref, small_ref, g_ref):
-    g_ref[G_AIR : G_AIR + 16, :] = q_ref[...]
-    g_ref[G_AIR + 16 : G_AIR + 32, :] = t_ref[...]
+def pack_gy_kernel(*refs):
+    given, kept = refs[:11], refs[11:20]
+    g_ref, side_ref, corner_ref, line_ref, sems = refs[20:]
+    copies = [
+        pltpu.make_async_copy(source, target, sems.at[n])
+        for n, (source, target) in enumerate(zip(given, (*kept, side_ref, corner_ref)))
+    ]
+    for n in (9, 10, 0, 1, 2, 3, 4, 5, 6, 7, 8):
+        copies[n].start()
+    copies[9].wait()
+    copies[10].wait()
+    line_ref[0:2, 0:48] = side_ref[0].astype(F32)
+    line_ref[2:6, 0:8] = corner_ref[0].astype(F32)
+    small = line_ref[0:1, :]
+    lane1 = lanes_of((1, 128))
+    for row, start in ((1, 48), (2, 96), (4, 104), (3, 112), (5, 120)):
+        small = jnp.where(lane1 < start, small, pltpu.roll(line_ref[row : row + 1, :], start, 1))
+    g_ref[G_LIST:G_ROWS, :] = jnp.broadcast_to(small, (8, 128))
+    copies[0].wait()
+    copies[1].wait()
     lane = lanes_of((8, 128))
     first = lane < 32
     low_level = lane % 32 < 16
-    for f, ref in enumerate((sz_ref, wt_ref, dn_ref, ox_ref, oy_ref, pm_ref)):
+    for f in range(FIELDS):
+        copies[2 + f].wait()
+        ref = kept[2 + f]
         parts = [ref[k * 16 : k * 16 + 16, :] for k in range(SD - 1, -1, -1)]
         block = jnp.concatenate(parts, 0)
         if f == 5:
             block = block.astype(F32)
         turned = jnp.transpose(block)
-        sides = []
-        for row in (127, 0):
+        out = []
+        for base, row in ((0, 127), (32, 0)):
             line = jnp.broadcast_to(turned[row : row + 1, :], (8, 128))
-            sides.append(line)
-        out = []
-        for n, line in enumerate(sides):
-            base = 32 * n
             line = pltpu.roll(line, 16, 1, stride=16, stride_axis=0)
             lev0 = pltpu.roll(line, base + 4, 1)
             lev1 = pltpu.roll(line, base + 12, 1)
             out.append(jnp.where(low_level, lev0, lev1))
-        g_ref[G_DROP + f * 8 : G_DROP + f * 8 + 8, :] = jnp.where(first, out[0], out[1])
-    g_ref[G_LIST : G_LIST + 8, :] = jnp.broadcast_to(small_ref[...], (8, 128))
+        block = jnp.where(first, out[0], out[1])
+        if f < 4:
+            air = kept[f // 2][8 * (f % 2) : 8 * (f % 2) + 8, :]
+            block = jnp.where(lane < 64, block, pltpu.roll(air, 67, 1))
+        g_ref[f * 8 : f * 8 + 8, :] = block
+    copies[8].wait()
 
 
 def pack_gx_kernel(
-    q_ref, t_ref, sz_ref, wt_ref, dn_ref, ox_ref, oy_ref, pm_ref, list_ref, south_ref, north_ref,
-    east_ref, west_ref,
+    q_ref, t_ref, sz_ref, wt_ref, dn_ref, ox_ref, oy_ref, pm_ref, list_ref, near_ref, far_ref,
+    east_ref, west_ref, rim_ref,
 ):
-    lane16 = lanes_of((16, 128))
-    ext = []
-    for a in range(2):
-        rows = slice(G_AIR + 16 * a, G_AIR + 16 * a + 16)
-        ext.append(jnp.where(lane16 < 64, north_ref[rows, :], south_ref[rows, :]))
+    even = lax.axis_index("gy") % 2 == 0
     lane = lanes_of((8, 128))
-    small = jnp.where(
-        (lane < 48) | ((lane >= 96) & (lane < 112)),
-        south_ref[G_LIST : G_LIST + 8, :],
-        north_ref[G_LIST : G_LIST + 8, :],
-    )
-    corners = []
+    slot = lane % 16
+    from_near = (((lane >= 32) & (lane < 64)) | (lane >= 67)) == even
+    blocks = []
     for f in range(FIELDS):
-        rows = slice(G_DROP + 8 * f, G_DROP + 8 * f + 8)
-        corners.append(jnp.where(lane < 32, south_ref[rows, :], north_ref[rows, :]))
-    refs = (sz_ref, wt_ref, dn_ref, ox_ref, oy_ref, pm_ref)
-    for side, (out_ref, i) in enumerate(((east_ref, 7), (west_ref, 0))):
-        for f, ref in enumerate(refs):
+        rows = slice(8 * f, 8 * f + 8)
+        merged = jnp.where(from_near, near_ref[rows, :], far_ref[rows, :])
+        rim_ref[rows, :] = merged
+        blocks.append(merged)
+    from_near = (((lane >= 48) & (lane < 96)) | (lane >= 112)) == even
+    small = jnp.where(from_near, near_ref[G_LIST:G_ROWS, :], far_ref[G_LIST:G_ROWS, :])
+    rim_ref[G_LIST:G_ROWS, :] = small
+    drops = (sz_ref, wt_ref, dn_ref, ox_ref, oy_ref, pm_ref)
+    for side, (out_ref, i, row) in enumerate(((east_ref, 7, 5), (west_ref, 0, 0))):
+        for f, ref in enumerate(drops):
             face = ref[pl.ds(i, 16, stride=8), :]
             if f == 5:
                 face = face.astype(F32)
-            out_ref[X_DROP + 16 * f : X_DROP + 16 * f + 16, :] = face
-            out_ref[X_CORNER + 8 * f : X_CORNER + 8 * f + 8, :] = corners[f]
-        out_ref[X_AIR : X_AIR + 16, :] = q_ref[...]
-        out_ref[X_AIR + 16 : X_AIR + 32, :] = t_ref[...]
-        out_ref[X_EXT : X_EXT + 16, :] = ext[0]
-        out_ref[X_EXT + 16 : X_EXT + 32, :] = ext[1]
-        out_ref[X_LIST : X_LIST + 8, :] = list_ref[side].astype(F32)
-        out_ref[X_SMALL : X_SMALL + 8, :] = small
-
-
-def departed_kernel(list_ref, small_ref, mask_ref):
-    entries = jnp.concatenate(
-        [list_ref[0, r : r + 1, :] for r in range(8)]
-        + [list_ref[1, r : r + 1, :] for r in range(8)]
-        + [small_ref[...].astype(I32)],
-        1,
-    )
-    width = entries.shape[1]
-    index = rows_of((128, width))
-    row = jnp.broadcast_to(entries >> 7, (128, width))
-    column = jnp.broadcast_to(entries & 127, (128, width))
-    one_row = jnp.where(row == index, 1.0, 0.0).astype(jnp.bfloat16)
-    one_column = jnp.where(column == index, 1.0, 0.0).astype(jnp.bfloat16)
-    mask_ref[...] = lax.dot_general(
-        one_row, one_column, (((1,), (1,)), ((), ())), preferred_element_type=F32
-    )
+            out_ref[16 * f : 16 * f + 16, :] = face
+        for g in range(4):
+            ref = (q_ref, t_ref)[g // 2]
+            at = 8 * (g % 2) + row
+            out_ref[X_AIR + 3 * g : X_AIR + 3 * g + 3, :] = ref[at : at + 3, :]
+        out_ref[X_AIR + 12 : X_AIR + 16, :] = jnp.zeros((4, 128), F32)
+        corner = small
+        for g in range(4):
+            here = (lane >= 64 + 8 * g) & (lane < 72 + 8 * g)
+            corner = jnp.where(here, shift(blocks[g], 8 * g, 1), corner)
+        for f in range(FIELDS):
+            here = (lane < 64) & (slot == f)
+            corner = jnp.where(here, shift(blocks[f], f - 4 - i, 1), corner)
+        out_ref[X_CORNER : X_CORNER + 8, :] = corner
+        for c in range(8):
+            piece = list_ref[0, side : side + 1, 128 * c : 128 * c + 128]
+            out_ref[X_LIST + c : X_LIST + c + 1, :] = piece.astype(F32)
+
+
+def one_hot(values, rows):
+    shape = (rows, values.shape[1])
+    hit = jnp.broadcast_to(values, shape) == rows_of(shape)
+    return jnp.where(hit, 1.0, 0.0).astype(jnp.bfloat16)
+
+
+def counts(rows, columns):
+    return lax.dot_general(rows, columns, (((1,), (1,)), ((), ())), preferred_element_type=F32)
+
+
+def departed_kernel(list_ref, g_ref, mask_ref):
+    entry = g_ref[G_LIST : G_LIST + 1, :].astype(I32)
+    mask_ref[...] = counts(one_hot(entry >> 7, 128), one_hot(entry & 127, 128))
+    for side, i in ((0, 7), (1, 0)):
+        entry = list_ref[0, side : side + 1, :]
+        found = counts(one_hot(entry >> 10, 16), one_hot(entry & 127, 128))
+        rows = pl.ds(i, 16, stride=8)
+        mask_ref[rows, :] = mask_ref[rows, :] + found
 
 
 def kernel_weights(offset):
@@ -187,10 +214,6 @@
     return out_radius, out_mult
 
 
-def shift(x, amount, axis):
-    return pltpu.roll(x, amount % x.shape[axis], axis)
-
-
 def droplets(windows, size, mult, dry, east, north, order):
     deposit = [[None] * 3 for _ in range(3)]
     grown = []
@@ -215,32 +238,27 @@
 
 def physics_kernel(
     q_ref, t_ref, sz_ref, wt_ref, dn_ref, ox_ref, oy_ref, pm_ref, mask_ref,
-    south_ref, north_ref, west_ref, east_ref,
+    rim_ref, west_ref, east_ref,
     moist_ref, warm_ref, size_ref, mult_ref, record_ref, box_ref,
-    halo_ref, table_ref,
+    halo_ref, table_ref, air_ref,
 ):
-    lane16 = lanes_of((16, 128))
     lane = lanes_of((8, 128))
     row8 = rows_of((8, 128))
     slot = lane % 16
 
     air = []
     for a, own_ref in enumerate((q_ref, t_ref)):
-        g_rows = slice(G_AIR + 16 * a, G_AIR + 16 * a + 16)
-        ext = jnp.where(lane16 < 64, north_ref[g_rows, :], south_ref[g_rows, :])
         levels = []
         for l in range(2):
-            rows = []
-            for ref in (west_ref, None, east_ref):
-                if ref is None:
-                    main = own_ref[8 * l : 8 * l + 8, :]
-                    side = ext[8 * l : 8 * l + 8, :]
-                else:
-                    base = 16 * a + 8 * l
-                    main = ref[X_AIR + base : X_AIR + base + 8, :]
-                    side = ref[X_EXT + base : X_EXT + base + 8, :]
-                rows.append(jnp.concatenate([main, side], 1))
-            levels.append(jnp.concatenate(rows, 0))
+            g = 2 * a + l
+            row = X_AIR + 3 * g
+            air_ref[g, 8:16, :128] = own_ref[8 * l : 8 * l + 8, :]
+            air_ref[g, 8:16, 128:] = shift(rim_ref[8 * g : 8 * g + 8, :], -67, 1)
+            air_ref[g, 5:8, :128] = west_ref[row : row + 3, :]
+            air_ref[g, 0:8, 128:] = shift(west_ref[X_CORNER : X_CORNER + 8, :], -67 - 8 * g, 1)
+            air_ref[g, 16:19, :128] = east_ref[row : row + 3, :]
+            air_ref[g, 16:24, 128:] = shift(east_ref[X_CORNER : X_CORNER + 8, :], -67 - 8 * g, 1)
+            levels.append(air_ref[g])
         air.append(levels)
     mixed = []
     for a in range(2):
@@ -277,18 +295,19 @@
 
     beyond = []
     for f in range(FIELDS):
-        c_rows = slice(X_CORNER + 8 * f, X_CORNER + 8 * f + 8)
-        g_rows = slice(G_DROP + 8 * f, G_DROP + 8 * f + 8)
-        own = jnp.where(lane < 32, south_ref[g_rows, :], north_ref[g_rows, :])
         line = jnp.where(
             slot == 3,
-            shift(west_ref[c_rows, :], -8, 1),
-            jnp.where(slot == 12, shift(east_ref[c_rows, :], 8, 1), own),
+            shift(west_ref[X_CORNER : X_CORNER + 8, :], 3 - f, 1),
+            jnp.where(
+                slot == 12,
+                shift(east_ref[X_CORNER : X_CORNER + 8, :], 12 - f, 1),
+                rim_ref[8 * f : 8 * f + 8, :],
+            ),
         )
         line = jnp.where((lane < 64) & (slot >= 3) & (slot <= 12), line, 0.0 if f == 5 else 0.5)
         beyond.append(line)
         for l in range(2):
-            base = X_DROP + 16 * f + l
+            base = 16 * f + l
             halo_ref[f, pl.ds(l, 8, stride=8), :] = west_ref[pl.ds(base, 8, stride=2), :]
             halo_ref[f, pl.ds(2 + l, 8, stride=8), :] = east_ref[pl.ds(base, 8, stride=2), :]
         for r in range(4, 8):
@@ -374,17 +393,12 @@
                 record_ref[n, 0:1, at : at + 128] = picked[n][c : c + 1, :]
             box_ref[0:1, at : at + 128] = box[c : c + 1, :]
 
-    own_small = jnp.where(
-        (lane < 48) | ((lane >= 96) & (lane < 112)),
-        south_ref[G_LIST : G_LIST + 8, :],
-        north_ref[G_LIST : G_LIST + 8, :],
-    )
     diagonal = lane >= 96
     by_west = diagonal & (lane % 16 < 8)
     entry = jnp.where(
         by_west,
-        west_ref[X_SMALL : X_SMALL + 8, :],
-        jnp.where(diagonal, east_ref[X_SMALL : X_SMALL + 8, :], own_small),
+        west_ref[X_CORNER : X_CORNER + 8, :],
+        jnp.where(diagonal, east_ref[X_CORNER : X_CORNER + 8, :], rim_ref[G_LIST:G_ROWS, :]),
     ).astype(I32)
     live = entry >= 0
     north_side = ((lane >= 48) & (lane < 96)) | (lane >= 112)
@@ -408,24 +422,27 @@
         record_ref[n, 0:1, 2048:2176] = line
 
 
-def whole(count):
-    return [pl.BlockSpec(memory_space=pltpu.VMEM)] * count
-
-
-def call(kernel, outs, args, scratch=(), flops=1 << 20):
+def call(kernel, outs, args, scratch=()):
     return pl.pallas_call(
         kernel,
         out_shape=outs,
-        in_specs=whole(len(args)),
+        in_specs=[pl.BlockSpec(memory_space=pltpu.VMEM)] * len(args),
         out_specs=jax.tree.map(lambda _: pl.BlockSpec(memory_space=pltpu.VMEM), outs),
         scratch_shapes=list(scratch),
-        cost_estimate=pl.CostEstimate(flops=flops, bytes_accessed=1 << 18, transcendentals=0),
+        compiler_params=pltpu.CompilerParams(vmem_limit_bytes=8 << 20),
+        cost_estimate=pl.CostEstimate(flops=1 << 20, bytes_accessed=1 << 18, transcendentals=0),
     )(*args)
 
 
 def ring(axis, step):
     count = lax.axis_size(axis)
     return [(i, (i + step) % count) for i in range(count)]
+
+
+def swaps(axis, first):
+    count = lax.axis_size(axis)
+    pairs = [(i % count, (i + 1) % count) for i in range(first, count, 2)]
+    return pairs + [(target, source) for source, target in pairs]
 
 
 def per_device(
@@ -456,26 +473,31 @@
             encounter_permutation,
         )
     )
-    long_lists = departing_eastwest_lists.reshape(2, 8, 128)
-    corner = departing_diagonal_lists[0]
-    small = (
-        jnp.concatenate(
-            [departing_northsouth_lists.reshape(-1), corner[0], corner[2], corner[1], corner[3]]
-        )
-        .astype(F32)
-        .reshape(1, 128)
-    )
-    to_gy = call(pack_gy_kernel, f32(G_ROWS, 128), (*air, *drops, small))
-    from_south = lax.ppermute(to_gy, "gy", ring("gy", 1))
-    from_north = lax.ppermute(to_gy, "gy", ring("gy", -1))
-    to_east, to_west = call(
+    given = (*air, *drops, departing_eastwest_lists)
+    short = (departing_northsouth_lists, departing_diagonal_lists)
+    *given, east_west, to_gy = pl.pallas_call(
+        pack_gy_kernel,
+        out_shape=(*(pltpu.VMEM(x.shape, x.dtype) for x in given), pltpu.VMEM((G_ROWS, 128), F32)),
+        in_specs=[pl.BlockSpec(memory_space=pltpu.HBM)] * 11,
+        out_specs=(pl.BlockSpec(memory_space=pltpu.VMEM),) * 10,
+        scratch_shapes=(
+            *(pltpu.VMEM(x.shape, x.dtype) for x in short),
+            pltpu.VMEM((8, 128), F32),
+            pltpu.SemaphoreType.DMA((11,)),
+        ),
+        compiler_params=pltpu.CompilerParams(vmem_limit_bytes=8 << 20),
+        cost_estimate=pl.CostEstimate(flops=1 << 20, bytes_accessed=1 << 18, transcendentals=0),
+    )(*(pltpu.with_memory_space_constraint(x, pltpu.HBM) for x in (*given, *short)))
+    far = lax.ppermute(to_gy, "gy", swaps("gy", 1))
+    near = lax.ppermute(to_gy, "gy", swaps("gy", 0))
+    departed = call(departed_kernel, f32(128, 128), (east_west, to_gy))
+    to_east, to_west, rim = call(
         pack_gx_kernel,
-        (f32(X_ROWS, 128), f32(X_ROWS, 128)),
-        (*air, *drops, long_lists, from_south, from_north),
+        (f32(X_ROWS, 128), f32(X_ROWS, 128), f32(G_ROWS, 128)),
+        (*given, east_west, near, far),
     )
     from_west = lax.ppermute(to_east, "gx", ring("gx", 1))
     from_east = lax.ppermute(to_west, "gx", ring("gx", -1))
-    departed = call(departed_kernel, f32(128, 128), (long_lists, small))
     moist, warm, size, mult, records, box = call(
         physics_kernel,
         (
@@ -486,8 +508,8 @@
             f32(5, 1, 2176),
             jax.ShapeDtypeStruct((1, 2176), I32),
         ),
-        (*air, *drops, departed, from_south, from_north, from_west, from_east),
-        scratch=(pltpu.VMEM((FIELDS, 64, 128), F32), pltpu.VMEM((2, 64, 128), F32)),
+        (*given, departed, rim, from_west, from_east),
+        scratch=(pltpu.VMEM((FIELDS, 64, 128), F32), pltpu.VMEM((2, 64, 128), F32), pltpu.VMEM((4, 24, 256), F32)),
     )
     return (
         moist.reshape(moisture_ratio.shape),

time: 43.9 us -> 33.6 us (0.77)
  the two profiles are of different devices: /device:TPU:8 before, /device:TPU:1 now
where the time goes in v2:
time: 33.6 us; the launch traced here: 33.3 us
  starting transfers between devices  26 us (77%)
  Pallas kernels  4.8 us (14%)
  waiting for transfers between devices  1.86 us (6%)
  between operations  0.69 us (2%)
    ppermute x1, starting transfers between devices, per_device(): from_east = lax.ppermute(to_west, 'gx', ring('gx', -1))  12.6 us
    ppermute x1, starting transfers between devices, per_device(): near = lax.ppermute(to_gy, 'gy', swaps('gy', 0))  6.08 us
    ppermute x1, starting transfers between devices, per_device(): far = lax.ppermute(to_gy, 'gy', swaps('gy', 1))  4.58 us
    ppermute x1, starting transfers between devices, per_device(): from_west = lax.ppermute(to_east, 'gx', ring('gx', 1))  2.72 us
    pallas_call x1, Pallas kernels, per_device(): pl.pallas_call(pack_gy_kernel, out_shape=(*(pltpu.VMEM(x.shape, x.dtype)...  2.49 us
    pallas_call x3, Pallas kernels, call(): pl.pallas_call(kernel, out_shape=outs, in_specs=[pl.BlockSpec(memory_spac...  2.3 us
    ppermute x1, waiting for transfers between devices, per_device(): from_east = lax.ppermute(to_west, 'gx', ring('gx', -1))  1.04 us
    ppermute x1, waiting for transfers between devices, per_device(): near = lax.ppermute(to_gy, 'gy', swaps('gy', 0))  0.82 us
  transfers between devices with their start and end apart: 4, of which 2 were waited for; matrix products, arithmetic and copies ran while one was open for 0% of the time, Pallas kernels for 1%

profile of v2, /device:TPU:1, one launch (start us, length us, event | category | flops | bytes accessed | tf_op | source)
XLA Modules:
  0.0 33.3 jit_solution(6999490683161940680)
XLA Ops:
  0.6 2.5 %shard_map.154 = (f32[16,128]{1,0:T(8,128)S(1)}, f32[16,128]{1,0:T(8,128)S(1)}, f32[128,128]{1,0:T(8,128)S(1)}, f32[128,128]{1,0:T(8,128)S(1)}, f32[128,128]{1,0...) custom-call(f32[16,128]{1,0:T(8,128)} %bitcast.18, ...), custom_call_target="tpu_custom_call" | custom-call | flops 1048576 | bytes 262144 | tf_op jit(solution)/shard_map/pallas_call | solution.py:478
  3.1 4.6 %collective-permute-start.1 = (f32[56,128]{1,0:T(8,128)S(1)}, f32[56,128]{1,0:T(8,128)S(1)}, u32[]{:S(2)}, u32[]{:S(2)}) collective-permute-start(f32[56,128]{1,0:T(8,128)S(1)} %get-tuple-element.34.g_ref), channel_id=1, source_target_pairs={{1,2},{3,4},{5,6},{7,0},{2,1},{4,3},{6,5},{0,7},{9,10},{11,12},{13... | collective-permute-start | bytes 86024 | tf_op jit(solution)/shard_map/ppermute | solution.py:491
  7.7 6.1 %collective-permute-start = (f32[56,128]{1,0:T(8,128)S(1)}, f32[56,128]{1,0:T(8,128)S(1)}, u32[]{:S(2)}, u32[]{:S(2)}) collective-permute-start(f32[56,128]{1,0:T(8,128)S(1)} %get-tuple-element.34.g_ref), channel_id=1, source_target_pairs={{0,1},{2,3},{4,5},{6,7},{1,0},{3,2},{5,4},{7,6},{8,9},{10,11},{12,... | collective-permute-start | bytes 86024 | tf_op jit(solution)/shard_map/ppermute | solution.py:492
  13.8 0.0 collective-permute-done.1.far_ref
  13.8 0.8 %collective-permute-done.near_ref = f32[56,128]{1,0:T(8,128)S(1)} collective-permute-done((f32[56,128]{1,0:T(8,128)S(1)}, f32[56,128]{1,0:T(8,128)S(1)}, u32[]{:S(2)}, u32[]{:S(2)}) %collective-permute-start) | collective-permute-done | bytes 28704 | tf_op jit(solution)/shard_map/ppermute | solution.py:492
  14.7 0.1 shard_map.156
  14.8 2.7 %collective-permute-start.2 = (f32[128,128]{1,0:T(8,128)S(1)}, f32[128,128]{1,0:T(8,128)S(1)}, u32[]{:S(2)}, u32[]{:S(2)}) collective-permute-start(f32[128,128]{1,0:T(8,128)S(1)} %get-tuple-element.36), channel_id=1, source_target_pairs={{0,8},{8,16},{16,24},{24,32},{32,40},{40,48},{48,56},{56,64},{64,7... | collective-permute-start | bytes 196616 | tf_op jit(solution)/shard_map/ppermute | solution.py:499
  17.5 12.6 %collective-permute-start.3 = (f32[128,128]{1,0:T(8,128)S(1)}, f32[128,128]{1,0:T(8,128)S(1)}, u32[]{:S(2)}, u32[]{:S(2)}) collective-permute-start(f32[128,128]{1,0:T(8,128)S(1)} %get-tuple-element.37), channel_id=1, source_target_pairs={{0,504},{8,0},{16,8},{24,16},{32,24},{40,32},{48,40},{56,48},{64,5... | collective-permute-start | bytes 196616 | tf_op jit(solution)/shard_map/ppermute | solution.py:500
  30.1 0.3 shard_map.155.mask_ref
  30.4 0.0 collective-permute-done.2.west_ref
  30.4 1.0 %collective-permute-done.3.east_ref = f32[128,128]{1,0:T(8,128)S(1)} collective-permute-done((f32[128,128]{1,0:T(8,128)S(1)}, f32[128,128]{1,0:T(8,128)S(1)}, u32[]{:S(2)}, u32[]{:S(2)}) %collective-permute-start.3) | collective-permute-done | bytes 65568 | tf_op jit(solution)/shard_map/ppermute | solution.py:500
  31.4 1.9 %shard_map.157 = (f32[16,128]{1,0:T(8,128)}, f32[16,128]{1,0:T(8,128)}, f32[128,128]{1,0:T(8,128)}, f32[128,128]{1,0:T(8,128)}, f32[5,1,2176]{2,1,0:T(1,128)}, /*index=5*/s32[1,2176]{1,0:T(1,128)}) custom-call(f32[16,128]{1,0:T(8,128)S(1)} %get-tuple-element.25.q_ref, f32[16,128]{1,0:T(8,128)S(1)} %get-tuple-element.26.t_ref, ...), custom_call_target="tpu_custom_call" | custom-call | flops 1048576 | bytes 262144 | tf_op jit(solution)/shard_map/pallas_call | solution.py:426
Async XLA Ops:
  3.1 10.7 %collective-permute-start.1 = (f32[56,128]{1,0:T(8,128)S(1)}, f32[56,128]{1,0:T(8,128)S(1)}, u32[]{:S(2)}, u32[]{:S(2)}) collective-permute-start(f32[56,128]{1,0:T(8,128)S(1)} %get-tuple-element.34.g_ref), channel_id=1, source_target_pairs={{1,2},{3,4},{5,6},{7,0},{2,1},{4,3},{6,5},{0,7},{9,10},{11,12},{13... | collective-permute-start | bytes 86024 | tf_op jit(solution)/shard_map/ppermute | solution.py:491
  7.7 6.9 %collective-permute-start = (f32[56,128]{1,0:T(8,128)S(1)}, f32[56,128]{1,0:T(8,128)S(1)}, u32[]{:S(2)}, u32[]{:S(2)}) collective-permute-start(f32[56,128]{1,0:T(8,128)S(1)} %get-tuple-element.34.g_ref), channel_id=1, source_target_pairs={{0,1},{2,3},{4,5},{6,7},{1,0},{3,2},{5,4},{7,6},{8,9},{10,11},{12,... | collective-permute-start | bytes 86024 | tf_op jit(solution)/shard_map/ppermute | solution.py:492
  14.8 15.6 %collective-permute-start.2 = (f32[128,128]{1,0:T(8,128)S(1)}, f32[128,128]{1,0:T(8,128)S(1)}, u32[]{:S(2)}, u32[]{:S(2)}) collective-permute-start(f32[128,128]{1,0:T(8,128)S(1)} %get-tuple-element.36), channel_id=1, source_target_pairs={{0,8},{8,16},{16,24},{24,32},{32,40},{40,48},{48,56},{56,64},{64,7... | collective-permute-start | bytes 196616 | tf_op jit(solution)/shard_map/ppermute | solution.py:499
  17.5 13.9 %collective-permute-start.3 = (f32[128,128]{1,0:T(8,128)S(1)}, f32[128,128]{1,0:T(8,128)S(1)}, u32[]{:S(2)}, u32[]{:S(2)}) collective-permute-start(f32[128,128]{1,0:T(8,128)S(1)} %get-tuple-element.37), channel_id=1, source_target_pairs={{0,504},{8,0},{16,8},{24,16},{32,24},{40,32},{48,40},{56,48},{64,5... | collective-permute-start | bytes 196616 | tf_op jit(solution)/shard_map/ppermute | solution.py:500

commit v3 on v2

--- a/solution.py
+++ b/solution.py
@@ -49,10 +49,10 @@
         pltpu.make_async_copy(source, target, sems.at[n])
         for n, (source, target) in enumerate(zip(given, (*kept, side_ref, corner_ref)))
     ]
-    for n in (9, 10, 0, 1, 2, 3, 4, 5, 6, 7, 8):
-        copies[n].start()
-    copies[9].wait()
-    copies[10].wait()
+    for copy in copies:
+        copy.start()
+    for copy in copies:
+        copy.wait()
     line_ref[0:2, 0:48] = side_ref[0].astype(F32)
     line_ref[2:6, 0:8] = corner_ref[0].astype(F32)
     small = line_ref[0:1, :]
@@ -60,13 +60,10 @@
     for row, start in ((1, 48), (2, 96), (4, 104), (3, 112), (5, 120)):
         small = jnp.where(lane1 < start, small, pltpu.roll(line_ref[row : row + 1, :], start, 1))
     g_ref[G_LIST:G_ROWS, :] = jnp.broadcast_to(small, (8, 128))
-    copies[0].wait()
-    copies[1].wait()
     lane = lanes_of((8, 128))
     first = lane < 32
     low_level = lane % 32 < 16
     for f in range(FIELDS):
-        copies[2 + f].wait()
         ref = kept[2 + f]
         parts = [ref[k * 16 : k * 16 + 16, :] for k in range(SD - 1, -1, -1)]
         block = jnp.concatenate(parts, 0)
@@ -85,7 +82,6 @@
             air = kept[f // 2][8 * (f % 2) : 8 * (f % 2) + 8, :]
             block = jnp.where(lane < 64, block, pltpu.roll(air, 67, 1))
         g_ref[f * 8 : f * 8 + 8, :] = block
-    copies[8].wait()
 
 
 def pack_gx_kernel(
@@ -99,11 +95,13 @@
     blocks = []
     for f in range(FIELDS):
         rows = slice(8 * f, 8 * f + 8)
-        merged = jnp.where(from_near, near_ref[rows, :], far_ref[rows, :])
+        near = jnp.where(even, near_ref[1, rows, :], near_ref[0, rows, :])
+        merged = jnp.where(from_near, near, far_ref[rows, :])
         rim_ref[rows, :] = merged
         blocks.append(merged)
     from_near = (((lane >= 48) & (lane < 96)) | (lane >= 112)) == even
-    small = jnp.where(from_near, near_ref[G_LIST:G_ROWS, :], far_ref[G_LIST:G_ROWS, :])
+    near = jnp.where(even, near_ref[1, G_LIST:G_ROWS, :], near_ref[0, G_LIST:G_ROWS, :])
+    small = jnp.where(from_near, near, far_ref[G_LIST:G_ROWS, :])
     rim_ref[G_LIST:G_ROWS, :] = small
     drops = (sz_ref, wt_ref, dn_ref, ox_ref, oy_ref, pm_ref)
     for side, (out_ref, i, row) in enumerate(((east_ref, 7, 5), (west_ref, 0, 0))):
@@ -150,31 +148,17 @@
         mask_ref[rows, :] = mask_ref[rows, :] + found
 
 
-def kernel_weights(offset):
-    return (
-        jnp.maximum(0.5 - offset, 0.0),
-        1.0 - jnp.abs(offset - 0.5),
-        jnp.maximum(offset - 0.5, 0.0),
-    )
-
-
-def cube_root(x):
-    y = jnp.exp(jnp.log(x) * (1.0 / 3.0))
-    return y - (y * y * y - x) / (3.0 * y * y)
-
-
 def grow(size, dry, forcing):
     initial = size * size
     lowest = dry * dry
     solute = KAPPA_SOLUTE * lowest * dry
+    target = initial + GROWTH_STEP * forcing
+    upper = (2.5 * GROWTH_STEP) * solute
+    lower = (1.5 * GROWTH_STEP) * solute
     wetted = initial
     for _ in range(NEWTON):
-        root = lax.rsqrt(wetted)
-        inverse_square = root * root
-        inverse = inverse_square * root
-        residue = wetted - initial - GROWTH_STEP * (forcing + solute * inverse)
-        slope = 1.0 + (1.5 * GROWTH_STEP) * solute * (inverse * inverse_square)
-        wetted = jnp.maximum(wetted - residue / slope, lowest)
+        power = wetted * wetted * (wetted * lax.rsqrt(wetted))
+        wetted = jnp.maximum((target * power + upper * wetted) / (power + lower), lowest)
     return wetted
 
 
@@ -186,9 +170,10 @@
 
 
 def coalesce(grown, mult, order):
-    bits = [((o & 1) == 1, (o & 2) == 2, (o & 4) == 4) for o in order]
-    new_radius, new_mult = [], []
+    bits = [((o & 1) == 1, (o & 2) == 2, o >= 4) for o in order]
+    changed = []
     for pair in range(SD // 2):
+        first, second = order[2 * pair], order[2 * pair + 1]
         p, q = bits[2 * pair], bits[2 * pair + 1]
         r1, r2 = pick(grown, p), pick(grown, q)
         m1, m2 = pick(mult, p), pick(mult, q)
@@ -196,42 +181,56 @@
         hr, lr = jnp.where(big, r1, r2), jnp.where(big, r2, r1)
         hm, lm = jnp.where(big, m1, m2), jnp.where(big, m2, m1)
         total = r1 + r2
-        rate = COLLIDE_RATE * hm * total * total * jnp.abs(r1 * r1 - r2 * r2)
+        rate = COLLIDE_RATE * hm * (total * total) * jnp.abs(r1 * r1 - r2 * r2)
         chance = 1.0 - jnp.exp(-rate)
-        merged = cube_root(lr * lr * lr + chance * hr * hr * hr)
+        volume = lr * lr * lr + chance * (hr * hr * hr)
+        merged = jnp.exp2(jnp.log2(volume) * (1.0 / 3.0))
         reduced = hm - chance * lm
-        new_radius += [jnp.where(big, hr, merged), jnp.where(big, merged, hr)]
-        new_mult += [jnp.where(big, reduced, lm), jnp.where(big, lm, reduced)]
+        high, low = jnp.where(big, first, second), jnp.where(big, second, first)
+        changed.append((high, low, merged, reduced))
     out_radius, out_mult = [], []
     for target in range(SD):
-        r, m = new_radius[0], new_mult[0]
-        for position in range(1, SD):
-            hit = order[position] == target
-            r = jnp.where(hit, new_radius[position], r)
-            m = jnp.where(hit, new_mult[position], m)
+        r, m = grown[target], mult[target]
+        for high, low, merged, reduced in changed:
+            r = jnp.where(low == target, merged, r)
+            m = jnp.where(high == target, reduced, m)
         out_radius.append(r)
         out_mult.append(m)
     return out_radius, out_mult
 
 
 def droplets(windows, size, mult, dry, east, north, order):
-    deposit = [[None] * 3 for _ in range(3)]
+    lines = [(w[1], w[0] - w[1], w[2] - w[1]) for w in windows]
+    middle = lines[1]
+    below = [x - y for x, y in zip(lines[0], middle)]
+    above = [x - y for x, y in zip(lines[2], middle)]
+    total = [[None] * 3 for _ in range(3)]
     grown = []
     for k in range(SD):
-        wx, wy = kernel_weights(east[k]), kernel_weights(north[k])
-        forcing = -(CURVATURE / size[k])
-        for a in range(3):
-            line = wy[0] * windows[a][0] + wy[1] * windows[a][1] + wy[2] * windows[a][2]
-            forcing = forcing + wx[a] * line
+        dx, dy = east[k] - 0.5, north[k] - 0.5
+        ahead_x, ahead_y = dx > 0.0, dy > 0.0
+        along, across = jnp.abs(dx), jnp.abs(dy)
+        outer = [jnp.where(ahead_x, x, y) for x, y in zip(above, below)]
+        forcing = middle[0] + across * jnp.where(ahead_y, middle[2], middle[1])
+        forcing = forcing + along * (outer[0] + across * jnp.where(ahead_y, outer[2], outer[1]))
+        forcing = forcing - CURVATURE / size[k]
         wetted = grow(size[k], dry[k], forcing)
-        radius = jnp.sqrt(wetted)
+        radius = wetted * lax.rsqrt(wetted)
         condensed = mult[k] * (wetted * radius - size[k] * size[k] * size[k])
-        for a in range(3):
-            part = wx[a] * condensed
+        up_x, up_y = jnp.maximum(dx, 0.0), jnp.maximum(dy, 0.0)
+        down_x, down_y = up_x - dx, up_y - dy
+        row = (condensed, condensed * down_y, condensed * up_y)
+        for a, factor in enumerate((None, down_x, up_x)):
             for b in range(3):
-                term = part * wy[b]
-                deposit[a][b] = term if k == 0 else deposit[a][b] + term
+                term = row[b] if factor is None else row[b] * factor
+                total[a][b] = term if k == 0 else total[a][b] + term
         grown.append(radius)
+    total = [(t[1], t[0] - t[1] - t[2], t[2]) for t in total]
+    deposit = [
+        total[1],
+        tuple(x - y - z for x, y, z in zip(*total)),
+        total[2],
+    ]
     radius, coalesced = coalesce(grown, mult, order)
     return radius, coalesced, deposit
 
@@ -239,9 +238,17 @@
 def physics_kernel(
     q_ref, t_ref, sz_ref, wt_ref, dn_ref, ox_ref, oy_ref, pm_ref, mask_ref,
     rim_ref, west_ref, east_ref,
+    moist_out, warm_out, size_out, mult_out, record_out, box_out,
     moist_ref, warm_ref, size_ref, mult_ref, record_ref, box_ref,
-    halo_ref, table_ref, air_ref,
+    halo_ref, table_ref, air_ref, sems,
 ):
+    leaving = [
+        pltpu.make_async_copy(source, target, sems.at[n])
+        for n, (source, target) in enumerate((
+            (moist_ref, moist_out), (warm_ref, warm_out), (size_ref, size_out),
+            (mult_ref, mult_out), (record_ref, record_out), (box_ref, box_out),
+        ))
+    ]
     lane = lanes_of((8, 128))
     row8 = rows_of((8, 128))
     slot = lane % 16
@@ -252,12 +259,12 @@
         for l in range(2):
             g = 2 * a + l
             row = X_AIR + 3 * g
-            air_ref[g, 8:16, :128] = own_ref[8 * l : 8 * l + 8, :]
-            air_ref[g, 8:16, 128:] = shift(rim_ref[8 * g : 8 * g + 8, :], -67, 1)
-            air_ref[g, 5:8, :128] = west_ref[row : row + 3, :]
-            air_ref[g, 0:8, 128:] = shift(west_ref[X_CORNER : X_CORNER + 8, :], -67 - 8 * g, 1)
-            air_ref[g, 16:19, :128] = east_ref[row : row + 3, :]
-            air_ref[g, 16:24, 128:] = shift(east_ref[X_CORNER : X_CORNER + 8, :], -67 - 8 * g, 1)
+            air_ref[g, 4:12, :128] = own_ref[8 * l : 8 * l + 8, :]
+            air_ref[g, 4:12, 128:] = shift(rim_ref[8 * g : 8 * g + 8, :], -67, 1)
+            air_ref[g, 1:4, :128] = west_ref[row : row + 3, :]
+            air_ref[g, 1:4, 128:] = shift(west_ref[X_CORNER : X_CORNER + 8, :], -67 - 8 * g, 1)[5:8, :]
+            air_ref[g, 12:15, :128] = east_ref[row : row + 3, :]
+            air_ref[g, 12:15, 128:] = shift(east_ref[X_CORNER : X_CORNER + 8, :], -67 - 8 * g, 1)[0:3, :]
             levels.append(air_ref[g])
         air.append(levels)
     mixed = []
@@ -282,9 +289,8 @@
                       [c[:, :128] for c in columns],
                       [shift(c[:, :128], -1, 0) for c in columns]])
         ahead = shift(humid, 2, 1)
-        tall = lanes_of((24, 128))
-        near = jnp.where(tall < 8, ahead[:, :128], shift(ahead[:, 128:], 8, 1))
-        turned.append(near[4:20, :])
+        tall = lanes_of((16, 128))
+        turned.append(jnp.where(tall < 8, ahead[:, :128], shift(ahead[:, 128:], 8, 1)))
     strip = jnp.concatenate(turned + turned + turned + turned, 0)
     strip = jnp.transpose(strip)
     lane1 = lanes_of((1, 128))
@@ -313,26 +319,13 @@
         for r in range(4, 8):
             halo_ref[f, pl.ds(r, 8, stride=8), :] = line
 
-    deposits = []
-    for l in range(2):
-        windows = [[moved[l][a][b][8:16, :] for b in range(3)] for a in range(3)]
-        tiles = [
-            [ref[k * 16 + 8 * l : k * 16 + 8 * l + 8, :] for k in range(SD)]
-            for ref in (sz_ref, wt_ref, dn_ref, ox_ref, oy_ref, pm_ref)
-        ]
-        radius, coalesced, deposit = droplets(windows, *tiles)
-        for k in range(SD):
-            rows = slice(k * 16 + 8 * l, k * 16 + 8 * l + 8)
-            size_ref[rows, :] = radius[k]
-            mult_ref[rows, :] = jnp.where(mask_ref[rows, :] > 0.5, 0.0, coalesced[k])
-        deposits.append(deposit)
     windows = []
     for a in range(3):
         line = []
         for b in range(3):
             line.append(jnp.concatenate(
-                [moved[0][a][b][7:8, :], moved[1][a][b][7:8, :],
-                 moved[0][a][b][16:17, :], moved[1][a][b][16:17, :]] + [rim[b][a]] * 4, 0))
+                [moved[0][a][b][3:4, :], moved[1][a][b][3:4, :],
+                 moved[0][a][b][12:13, :], moved[1][a][b][12:13, :]] + [rim[b][a]] * 4, 0))
         windows.append(line)
     tiles = [[halo_ref[f, 8 * k : 8 * k + 8, :] for k in range(SD)] for f in range(5)]
     order = [halo_ref[5, 8 * k : 8 * k + 8, :].astype(I32) for k in range(SD)]
@@ -340,35 +333,6 @@
     for k in range(SD):
         table_ref[0, 8 * k : 8 * k + 8, :] = halo_radius[k]
         table_ref[1, 8 * k : 8 * k + 8, :] = halo_mult[k]
-
-    def along_y(d, a):
-        return (
-            d[a][1]
-            + jnp.where(lane == 0, 0.0, shift(d[a][2], 1, 1))
-            + jnp.where(lane == 127, 0.0, shift(d[a][0], -1, 1))
-        )
-
-    from_west = along_y(outer, 2)
-    from_east = along_y(outer, 0)
-    rim_line = [jnp.where(lane1 < 32, outer[a][2][4:5, :], outer[a][0][4:5, :]) for a in range(3)]
-    rim_line = shift(rim_line[2], 1, 1) + rim_line[1] + shift(rim_line[0], -1, 1)
-    rim_line = jnp.broadcast_to(rim_line, (8, 128))
-    for l in range(2):
-        own = [along_y(deposits[l], a) for a in range(3)]
-        west_row = jnp.broadcast_to(from_west[l : l + 1, :], (8, 128))
-        east_row = jnp.broadcast_to(from_east[2 + l : 3 + l, :], (8, 128))
-        source = (
-            own[1]
-            + jnp.where(row8 == 0, west_row, shift(own[2], 1, 0))
-            + jnp.where(row8 == 7, east_row, shift(own[0], -1, 0))
-        )
-        for side, j in enumerate((0, 127)):
-            wanted = lane == side * 32 + l * 16 + 4 + row8
-            column = jnp.sum(jnp.where(wanted, rim_line, 0.0), axis=1, keepdims=True)
-            source = source + jnp.where(lane == j, column, 0.0)
-        rows = slice(8 * l, 8 * l + 8)
-        moist_ref[rows, :] = mixed[0][l][8:16, :128] - VAPOUR_PER_SOURCE * source
-        warm_ref[rows, :] = mixed[1][l][8:16, :128] + WARMING_FACTOR * source
 
     for side, (ref, dx) in enumerate(((west_ref, 1), (east_ref, -1))):
         entry = ref[X_LIST : X_LIST + 8, :].astype(I32)
@@ -420,14 +384,65 @@
         got = jnp.take_along_axis(table, at, axis=1)
         line = jnp.sum(jnp.where(mine, got, 0.0), axis=0, keepdims=True)
         record_ref[n, 0:1, 2048:2176] = line
-
-
-def call(kernel, outs, args, scratch=()):
+    leaving[4].start()
+    leaving[5].start()
+
+    deposits = []
+    for l in range(2):
+        windows = [[moved[l][a][b][4:12, :] for b in range(3)] for a in range(3)]
+        tiles = [
+            [ref[k * 16 + 8 * l : k * 16 + 8 * l + 8, :] for k in range(SD)]
+            for ref in (sz_ref, wt_ref, dn_ref, ox_ref, oy_ref, pm_ref)
+        ]
+        radius, coalesced, deposit = droplets(windows, *tiles)
+        for k in range(SD):
+            rows = slice(k * 16 + 8 * l, k * 16 + 8 * l + 8)
+            size_ref[rows, :] = radius[k]
+            mult_ref[rows, :] = jnp.where(mask_ref[rows, :] > 0.5, 0.0, coalesced[k])
+        deposits.append(deposit)
+    leaving[2].start()
+    leaving[3].start()
+
+    def along_y(d, a):
+        return (
+            d[a][1]
+            + jnp.where(lane == 0, 0.0, shift(d[a][2], 1, 1))
+            + jnp.where(lane == 127, 0.0, shift(d[a][0], -1, 1))
+        )
+
+    from_west = along_y(outer, 2)
+    from_east = along_y(outer, 0)
+    rim_line = [jnp.where(lane1 < 32, outer[a][2][4:5, :], outer[a][0][4:5, :]) for a in range(3)]
+    rim_line = shift(rim_line[2], 1, 1) + rim_line[1] + shift(rim_line[0], -1, 1)
+    rim_line = jnp.broadcast_to(rim_line, (8, 128))
+    for l in range(2):
+        own = [along_y(deposits[l], a) for a in range(3)]
+        west_row = jnp.broadcast_to(from_west[l : l + 1, :], (8, 128))
+        east_row = jnp.broadcast_to(from_east[2 + l : 3 + l, :], (8, 128))
+        source = (
+            own[1]
+            + jnp.where(row8 == 0, west_row, shift(own[2], 1, 0))
+            + jnp.where(row8 == 7, east_row, shift(own[0], -1, 0))
+        )
+        for side, j in enumerate((0, 127)):
+            wanted = lane == side * 32 + l * 16 + 4 + row8
+            column = jnp.sum(jnp.where(wanted, rim_line, 0.0), axis=1, keepdims=True)
+            source = source + jnp.where(lane == j, column, 0.0)
+        rows = slice(8 * l, 8 * l + 8)
+        moist_ref[rows, :] = mixed[0][l][4:12, :128] - VAPOUR_PER_SOURCE * source
+        warm_ref[rows, :] = mixed[1][l][4:12, :128] + WARMING_FACTOR * source
+    leaving[0].start()
+    leaving[1].start()
+    for copy in leaving:
+        copy.wait()
+
+
+def call(kernel, outs, args, scratch=(), space=pltpu.VMEM):
     return pl.pallas_call(
         kernel,
         out_shape=outs,
         in_specs=[pl.BlockSpec(memory_space=pltpu.VMEM)] * len(args),
-        out_specs=jax.tree.map(lambda _: pl.BlockSpec(memory_space=pltpu.VMEM), outs),
+        out_specs=jax.tree.map(lambda _: pl.BlockSpec(memory_space=space), outs),
         scratch_shapes=list(scratch),
         compiler_params=pltpu.CompilerParams(vmem_limit_bytes=8 << 20),
         cost_estimate=pl.CostEstimate(flops=1 << 20, bytes_accessed=1 << 18, transcendentals=0),
@@ -489,7 +504,8 @@
         cost_estimate=pl.CostEstimate(flops=1 << 20, bytes_accessed=1 << 18, transcendentals=0),
     )(*(pltpu.with_memory_space_constraint(x, pltpu.HBM) for x in (*given, *short)))
     far = lax.ppermute(to_gy, "gy", swaps("gy", 1))
-    near = lax.ppermute(to_gy, "gy", swaps("gy", 0))
+    count = lax.axis_size("gy")
+    near = lax.all_gather(to_gy, "gy", axis_index_groups=[[i, i + 1] for i in range(0, count, 2)])
     departed = call(departed_kernel, f32(128, 128), (east_west, to_gy))
     to_east, to_west, rim = call(
         pack_gx_kernel,
@@ -498,18 +514,26 @@
     )
     from_west = lax.ppermute(to_east, "gx", ring("gx", 1))
     from_east = lax.ppermute(to_west, "gx", ring("gx", -1))
+    outs = (
+        f32(16, 128),
+        f32(16, 128),
+        f32(128, 128),
+        f32(128, 128),
+        f32(5, 1, 2176),
+        jax.ShapeDtypeStruct((1, 2176), I32),
+    )
     moist, warm, size, mult, records, box = call(
         physics_kernel,
-        (
-            f32(16, 128),
-            f32(16, 128),
-            f32(128, 128),
-            f32(128, 128),
-            f32(5, 1, 2176),
-            jax.ShapeDtypeStruct((1, 2176), I32),
+        outs,
+        (*given, departed, rim, from_west, from_east),
+        scratch=(
+            *(pltpu.VMEM(x.shape, x.dtype) for x in outs),
+            pltpu.VMEM((FIELDS, 64, 128), F32),
+            pltpu.VMEM((2, 64, 128), F32),
+            pltpu.VMEM((4, 16, 256), F32),
+            pltpu.SemaphoreType.DMA((6,)),
         ),
-        (*given, departed, rim, from_west, from_east),
-        scratch=(pltpu.VMEM((FIELDS, 64, 128), F32), pltpu.VMEM((2, 64, 128), F32), pltpu.VMEM((4, 24, 256), F32)),
+        space=pltpu.HBM,
     )
     return (
         moist.reshape(moisture_ratio.shape),

time: 33.6 us -> 31.8 us (0.946)
  blocking collectives: 0 us -> 5.67 us
  starting transfers between devices: 26 us -> 20.4 us
  Pallas kernels: 4.8 us -> 3.84 us
  waiting for transfers between devices: 1.86 us -> 1.04 us
    ppermute x1 -> x0, starting transfers between devices: 6.08 us -> none  [per_device(): near = lax.ppermute(to_gy, 'gy', swaps('gy', 0))]
    all_gather x0 -> x1, blocking collectives: none -> 5.67 us  [per_device(): lax.all_gather(to_gy, 'gy', axis_index_groups=[[i, i + 1] for i in range(...]
    pallas_call x1, Pallas kernels: 2.49 us -> 1.64 us  [per_device(): pl.pallas_call(pack_gy_kernel, out_shape=(*(pltpu.VMEM(x.shape, x.dtype)...]
    ppermute x1 -> x0, waiting for transfers between devices: 0.82 us -> none  [per_device(): near = lax.ppermute(to_gy, 'gy', swaps('gy', 0))]
    ppermute x1, starting transfers between devices: 2.72 us -> 3.19 us  [per_device(): from_west = lax.ppermute(to_east, 'gx', ring('gx', 1))]
  transfers between devices with their start and end apart: 4 -> 3, of which waited for: 2 -> 1; matrix products, arithmetic and copies ran while one was open for 0% -> 0% of each run, Pallas kernels for 1% -> 1%
where the time goes in v3:
time: 31.8 us; the launch traced here: 31.6 us
  starting transfers between devices  20.4 us (64%)
  blocking collectives  5.67 us (18%)
  Pallas kernels  3.84 us (12%)
  waiting for transfers between devices  1.04 us (3%)
  between operations  0.67 us (2%)
    ppermute x1, starting transfers between devices, per_device(): from_east = lax.ppermute(to_west, 'gx', ring('gx', -1))  12.6 us
    all_gather x1, blocking collectives, per_device(): lax.all_gather(to_gy, 'gy', axis_index_groups=[[i, i + 1] for i in range(...  5.67 us
    ppermute x1, starting transfers between devices, per_device(): far = lax.ppermute(to_gy, 'gy', swaps('gy', 1))  4.58 us
    ppermute x1, starting transfers between devices, per_device(): from_west = lax.ppermute(to_east, 'gx', ring('gx', 1))  3.19 us
    pallas_call x3, Pallas kernels, call(): pl.pallas_call(kernel, out_shape=outs, in_specs=[pl.BlockSpec(memory_spac...  2.2 us
    pallas_call x1, Pallas kernels, per_device(): pl.pallas_call(pack_gy_kernel, out_shape=(*(pltpu.VMEM(x.shape, x.dtype)...  1.64 us
    ppermute x1, waiting for transfers between devices, per_device(): from_east = lax.ppermute(to_west, 'gx', ring('gx', -1))  1.04 us
  transfers between devices with their start and end apart: 3, of which 1 were waited for; matrix products, arithmetic and copies ran while one was open for 0% of the time, Pallas kernels for 1%

profile of v3, /device:TPU:1, one launch (start us, length us, event | category | flops | bytes accessed | tf_op | source)
XLA Modules:
  0.0 31.6 jit_solution(7989025494124830259)
XLA Ops:
  0.6 1.6 %shard_map.154 = (f32[16,128]{1,0:T(8,128)S(1)}, f32[16,128]{1,0:T(8,128)S(1)}, f32[128,128]{1,0:T(8,128)S(1)}, f32[128,128]{1,0:T(8,128)S(1)}, f32[128,128]{1,0...) custom-call(f32[16,128]{1,0:T(8,128)} %bitcast.20, ...), custom_call_target="tpu_custom_call" | custom-call | flops 1048576 | bytes 262144 | tf_op jit(solution)/shard_map/pallas_call | solution.py:493
  2.3 4.6 %collective-permute-start = (f32[56,128]{1,0:T(8,128)S(1)}, f32[56,128]{1,0:T(8,128)S(1)}, u32[]{:S(2)}, u32[]{:S(2)}) collective-permute-start(f32[56,128]{1,0:T(8,128)S(1)} %get-tuple-element.34.g_ref), channel_id=1, source_target_pairs={{1,2},{3,4},{5,6},{7,0},{2,1},{4,3},{6,5},{0,7},{9,10},{11,12},{13... | collective-permute-start | bytes 86024 | tf_op jit(solution)/shard_map/ppermute | solution.py:506
  6.9 5.7 %all-gather = f32[112,128]{1,0:T(8,128)S(1)} all-gather(f32[56,128]{1,0:T(8,128)S(1)} %get-tuple-element.34.g_ref), channel_id=2, replica_groups={{0,1},{2,3},{4,5},{6,7},{8,9},{10,11},{12,13},{14,15},{16,17},{18,19},{..., dimensions={0}, use_global_device_ids=true | all-gather | bytes 86016 | tf_op jit(solution)/shard_map/all_gather | solution.py:508
  12.6 0.0 collective-permute-done.far_ref
  12.6 0.1 shard_map.156
  12.7 3.2 %collective-permute-start.1 = (f32[128,128]{1,0:T(8,128)S(1)}, f32[128,128]{1,0:T(8,128)S(1)}, u32[]{:S(2)}, u32[]{:S(2)}) collective-permute-start(f32[128,128]{1,0:T(8,128)S(1)} %get-tuple-element.36), channel_id=1, source_target_pairs={{0,8},{8,16},{16,24},{24,32},{32,40},{40,48},{48,56},{56,64},{64,7... | collective-permute-start | bytes 196616 | tf_op jit(solution)/shard_map/ppermute | solution.py:515
  15.9 12.6 %collective-permute-start.2 = (f32[128,128]{1,0:T(8,128)S(1)}, f32[128,128]{1,0:T(8,128)S(1)}, u32[]{:S(2)}, u32[]{:S(2)}) collective-permute-start(f32[128,128]{1,0:T(8,128)S(1)} %get-tuple-element.37), channel_id=1, source_target_pairs={{0,504},{8,0},{16,8},{24,16},{32,24},{40,32},{48,40},{56,48},{64,5... | collective-permute-start | bytes 196616 | tf_op jit(solution)/shard_map/ppermute | solution.py:516
  28.5 0.3 shard_map.155.mask_ref
  28.7 0.0 collective-permute-done.1.west_ref
  28.7 1.0 %collective-permute-done.2.east_ref = f32[128,128]{1,0:T(8,128)S(1)} collective-permute-done((f32[128,128]{1,0:T(8,128)S(1)}, f32[128,128]{1,0:T(8,128)S(1)}, u32[]{:S(2)}, u32[]{:S(2)}) %collective-permute-start.2) | collective-permute-done | bytes 65568 | tf_op jit(solution)/shard_map/ppermute | solution.py:516
  29.8 1.8 %shard_map.157 = (f32[16,128]{1,0:T(8,128)}, f32[16,128]{1,0:T(8,128)}, f32[128,128]{1,0:T(8,128)}, f32[128,128]{1,0:T(8,128)}, f32[5,1,2176]{2,1,0:T(1,128)}, /*index=5*/s32[1,2176]{1,0:T(1,128)}) custom-call(f32[16,128]{1,0:T(8,128)S(1)} %get-tuple-element.25.q_ref, f32[16,128]{1,0:T(8,128)S(1)} %get-tuple-element.26.t_ref, ...), custom_call_target="tpu_custom_call" | custom-call | flops 1048576 | bytes 262144 | tf_op jit(solution)/shard_map/pallas_call | solution.py:441
Async XLA Ops:
  2.3 10.3 %collective-permute-start = (f32[56,128]{1,0:T(8,128)S(1)}, f32[56,128]{1,0:T(8,128)S(1)}, u32[]{:S(2)}, u32[]{:S(2)}) collective-permute-start(f32[56,128]{1,0:T(8,128)S(1)} %get-tuple-element.34.g_ref), channel_id=1, source_target_pairs={{1,2},{3,4},{5,6},{7,0},{2,1},{4,3},{6,5},{0,7},{9,10},{11,12},{13... | collective-permute-start | bytes 86024 | tf_op jit(solution)/shard_map/ppermute | solution.py:506
  12.7 16.1 %collective-permute-start.1 = (f32[128,128]{1,0:T(8,128)S(1)}, f32[128,128]{1,0:T(8,128)S(1)}, u32[]{:S(2)}, u32[]{:S(2)}) collective-permute-start(f32[128,128]{1,0:T(8,128)S(1)} %get-tuple-element.36), channel_id=1, source_target_pairs={{0,8},{8,16},{16,24},{24,32},{32,40},{40,48},{48,56},{56,64},{64,7... | collective-permute-start | bytes 196616 | tf_op jit(solution)/shard_map/ppermute | solution.py:515
  15.9 13.9 %collective-permute-start.2 = (f32[128,128]{1,0:T(8,128)S(1)}, f32[128,128]{1,0:T(8,128)S(1)}, u32[]{:S(2)}, u32[]{:S(2)}) collective-permute-start(f32[128,128]{1,0:T(8,128)S(1)} %get-tuple-element.37), channel_id=1, source_target_pairs={{0,504},{8,0},{16,8},{24,16},{32,24},{40,32},{48,40},{56,48},{64,5... | collective-permute-start | bytes 196616 | tf_op jit(solution)/shard_map/ppermute | solution.py:516

commit v4 on v3

--- a/solution.py
+++ b/solution.py
@@ -235,9 +235,123 @@
     return radius, coalesced, deposit
 
 
-def physics_kernel(
-    q_ref, t_ref, sz_ref, wt_ref, dn_ref, ox_ref, oy_ref, pm_ref, mask_ref,
-    rim_ref, west_ref, east_ref,
+def mix(x, other):
+    across = shift(x, 1, 0) + shift(x, -1, 0) + shift(x, 1, 1) + shift(x, -1, 1) - 4.0 * x
+    return x + MIX_HORIZONTAL * across + MIX_VERTICAL * (other + x - 2.0 * x)
+
+
+def moisture_excess(vapour, warm):
+    most = EXCESS_FACTOR * jnp.exp(17.27 * (warm - 273.15) / (warm - 35.86))
+    return vapour / most - 1.0
+
+
+def stencil(humid):
+    columns = [shift(humid, 1, 1)[:, :128], humid[:, :128], shift(humid, -1, 1)[:, :128]]
+    return [[shift(c, 1, 0) for c in columns], columns, [shift(c, -1, 0) for c in columns]]
+
+
+def along_y(d, a):
+    lane = lanes_of((8, 128))
+    return (
+        d[a][1]
+        + jnp.where(lane == 0, 0.0, shift(d[a][2], 1, 1))
+        + jnp.where(lane == 127, 0.0, shift(d[a][0], -1, 1))
+    )
+
+
+def face_records(list_rows, step, first_row, table_ref, halo_ref, record_ref, box_ref):
+    entry = list_rows.astype(I32)
+    live = entry >= 0
+    column = entry & 127
+    group = entry >> 10
+    picked = [jnp.zeros((8, 128), F32) for _ in range(5)]
+    for k in range(SD):
+        for l in range(2):
+            here = live & (group == 2 * k + l)
+            r = 8 * k + first_row + l
+            for n in range(5):
+                src = table_ref if n < 2 else halo_ref
+                line = jnp.broadcast_to(src[n, r : r + 1, :], (8, 128))
+                got = jnp.take_along_axis(line, column, axis=1)
+                picked[n] = jnp.where(here, got, picked[n])
+    box = (((entry >> 10) & 1) * 8 + (((entry >> 7) + step) & 7)) * 128 + column
+    box = jnp.where(live, box, -1)
+    for c in range(8):
+        lanes = slice(c * 128, c * 128 + 128)
+        for n in range(5):
+            record_ref[n, 0:1, lanes] = picked[n][c : c + 1, :]
+        box_ref[0:1, lanes] = box[c : c + 1, :]
+
+
+def west_kernel(
+    q_ref, t_ref, sz_ref, wt_ref, dn_ref, ox_ref, oy_ref, pm_ref, mask_ref, rim_ref, west_ref,
+    size_ref, mult_ref, humid_ref, mixed_ref, source_ref, record_ref, box_ref,
+    halo_ref, table_ref, air_ref,
+):
+    row8 = rows_of((8, 128))
+    for a, own_ref in enumerate((q_ref, t_ref)):
+        for l in range(2):
+            g = 2 * a + l
+            row = X_AIR + 3 * g
+            side = shift(west_ref[X_CORNER : X_CORNER + 8, :], -67 - 8 * g, 1)
+            air_ref[g, 4:12, :128] = own_ref[8 * l : 8 * l + 8, :]
+            air_ref[g, 4:12, 128:] = shift(rim_ref[8 * g : 8 * g + 8, :], -67, 1)
+            air_ref[g, 1:4, :128] = west_ref[row : row + 3, :]
+            air_ref[g, 1:4, 128:] = side[5:8, :]
+    moved = []
+    for l in range(2):
+        vapour = mix(air_ref[l], air_ref[1 - l])
+        warm = mix(air_ref[2 + l], air_ref[3 - l])
+        mixed_ref[8 * l : 8 * l + 8, :] = vapour[4:12, :128]
+        mixed_ref[16 + 8 * l : 24 + 8 * l, :] = warm[4:12, :128]
+        humid = moisture_excess(vapour, warm)
+        humid_ref[8 * l : 8 * l + 8, :] = humid[0:8, :]
+        moved.append(stencil(humid))
+
+    for f in range(FIELDS):
+        for r in range(8):
+            halo_ref[f, pl.ds(r, 8, stride=8), :] = west_ref[pl.ds(16 * f + r % 2, 8, stride=2), :]
+    windows = [
+        [
+            jnp.concatenate([moved[0][a][b][3:4, :], moved[1][a][b][3:4, :]] * 4, 0)
+            for b in range(3)
+        ]
+        for a in range(3)
+    ]
+    tiles = [[halo_ref[f, 8 * k : 8 * k + 8, :] for k in range(SD)] for f in range(5)]
+    order = [halo_ref[5, 8 * k : 8 * k + 8, :].astype(I32) for k in range(SD)]
+    halo_radius, halo_mult, outer = droplets(windows, *tiles, order)
+    for k in range(SD):
+        table_ref[0, 8 * k : 8 * k + 8, :] = halo_radius[k]
+        table_ref[1, 8 * k : 8 * k + 8, :] = halo_mult[k]
+    face_records(
+        west_ref[X_LIST : X_LIST + 8, :], 1, 0, table_ref, halo_ref, record_ref, box_ref
+    )
+
+    from_west = along_y(outer, 2)
+    for l in range(2):
+        windows = [[moved[l][a][b][4:12, :] for b in range(3)] for a in range(3)]
+        tiles = [
+            [ref[k * 16 + 8 * l : k * 16 + 8 * l + 8, :] for k in range(SD)]
+            for ref in (sz_ref, wt_ref, dn_ref, ox_ref, oy_ref, pm_ref)
+        ]
+        radius, coalesced, deposit = droplets(windows, *tiles)
+        for k in range(SD):
+            rows = slice(k * 16 + 8 * l, k * 16 + 8 * l + 8)
+            size_ref[rows, :] = radius[k]
+            mult_ref[rows, :] = jnp.where(mask_ref[rows, :] > 0.5, 0.0, coalesced[k])
+        own = [jnp.where(row8 < 6, along_y(deposit, a), 0.0) for a in range(3)]
+        west_row = jnp.broadcast_to(from_west[l : l + 1, :], (8, 128))
+        source_ref[8 * l : 8 * l + 8, :] = (
+            own[1]
+            + jnp.where(row8 == 0, west_row, shift(own[2], 1, 0))
+            + jnp.where(row8 == 7, 0.0, shift(own[0], -1, 0))
+        )
+
+
+def east_kernel(
+    q_ref, t_ref, sz_ref, wt_ref, dn_ref, ox_ref, oy_ref, pm_ref, mask_ref, rim_ref, west_ref,
+    east_ref, early_size, early_mult, humid_ref, mixed_ref, source_ref, west_record, west_box,
     moist_out, warm_out, size_out, mult_out, record_out, box_out,
     moist_ref, warm_ref, size_ref, mult_ref, record_ref, box_ref,
     halo_ref, table_ref, air_ref, sems,
@@ -245,62 +359,48 @@
     leaving = [
         pltpu.make_async_copy(source, target, sems.at[n])
         for n, (source, target) in enumerate((
-            (moist_ref, moist_out), (warm_ref, warm_out), (size_ref, size_out),
-            (mult_ref, mult_out), (record_ref, record_out), (box_ref, box_out),
+            (west_record, record_out.at[:, :, 0:1024]), (west_box, box_out.at[:, 0:1024]),
+            (size_ref, size_out), (mult_ref, mult_out),
+            (record_ref, record_out.at[:, :, 1024:2176]), (box_ref, box_out.at[:, 1024:2176]),
+            (moist_ref, moist_out), (warm_ref, warm_out),
         ))
     ]
+    leaving[0].start()
+    leaving[1].start()
     lane = lanes_of((8, 128))
+    lane1 = lanes_of((1, 128))
     row8 = rows_of((8, 128))
     slot = lane % 16
-
-    air = []
     for a, own_ref in enumerate((q_ref, t_ref)):
-        levels = []
         for l in range(2):
             g = 2 * a + l
             row = X_AIR + 3 * g
-            air_ref[g, 4:12, :128] = own_ref[8 * l : 8 * l + 8, :]
-            air_ref[g, 4:12, 128:] = shift(rim_ref[8 * g : 8 * g + 8, :], -67, 1)
-            air_ref[g, 1:4, :128] = west_ref[row : row + 3, :]
-            air_ref[g, 1:4, 128:] = shift(west_ref[X_CORNER : X_CORNER + 8, :], -67 - 8 * g, 1)[5:8, :]
-            air_ref[g, 12:15, :128] = east_ref[row : row + 3, :]
-            air_ref[g, 12:15, 128:] = shift(east_ref[X_CORNER : X_CORNER + 8, :], -67 - 8 * g, 1)[0:3, :]
-            levels.append(air_ref[g])
-        air.append(levels)
+            side = shift(east_ref[X_CORNER : X_CORNER + 8, :], -67 - 8 * g, 1)
+            air_ref[g, 0:5, :128] = own_ref[8 * l + 3 : 8 * l + 8, :]
+            air_ref[g, 0:5, 128:] = shift(rim_ref[8 * g : 8 * g + 8, :], -67, 1)[3:8, :]
+            air_ref[g, 5:8, :128] = east_ref[row : row + 3, :]
+            air_ref[g, 5:8, 128:] = side[0:3, :]
     mixed = []
-    for a in range(2):
-        both = []
-        for l in range(2):
-            x = air[a][l]
-            other = air[a][1 - l]
-            across = (
-                shift(x, 1, 0) + shift(x, -1, 0) + shift(x, 1, 1) + shift(x, -1, 1) - 4.0 * x
-            )
-            both.append(x + MIX_HORIZONTAL * across + MIX_VERTICAL * (other + x - 2.0 * x))
-        mixed.append(both)
     moved = []
     turned = []
     for l in range(2):
-        vapour, warm = mixed[0][l], mixed[1][l]
-        most = EXCESS_FACTOR * jnp.exp(17.27 * (warm - 273.15) / (warm - 35.86))
-        humid = vapour / most - 1.0
-        columns = [shift(humid, 1, 1), humid, shift(humid, -1, 1)]
-        moved.append([[shift(c[:, :128], 1, 0) for c in columns],
-                      [c[:, :128] for c in columns],
-                      [shift(c[:, :128], -1, 0) for c in columns]])
-        ahead = shift(humid, 2, 1)
+        vapour = mix(air_ref[l], air_ref[1 - l])
+        warm = mix(air_ref[2 + l], air_ref[3 - l])
+        mixed.append((shift(vapour[:, :128], 3, 0), shift(warm[:, :128], 3, 0)))
+        humid = moisture_excess(vapour, warm)
+        moved.append(stencil(humid))
+        whole = jnp.concatenate([humid_ref[8 * l : 8 * l + 8, :], shift(humid, -1, 0)], 0)
+        ahead = shift(whole, 2, 1)
         tall = lanes_of((16, 128))
         turned.append(jnp.where(tall < 8, ahead[:, :128], shift(ahead[:, 128:], 8, 1)))
-    strip = jnp.concatenate(turned + turned + turned + turned, 0)
-    strip = jnp.transpose(strip)
-    lane1 = lanes_of((1, 128))
+    strip = jnp.transpose(jnp.concatenate(turned * 4, 0))
     rim = []
     for b in range(3):
         line = jnp.where(lane1 < 32, strip[b : b + 1, :], strip[b + 9 : b + 10, :])
         rim.append([shift(line, 1, 1), line, shift(line, -1, 1)])
 
     beyond = []
-    for f in range(FIELDS):
+    for f, own_ref in enumerate((sz_ref, wt_ref, dn_ref, ox_ref, oy_ref, pm_ref)):
         line = jnp.where(
             slot == 3,
             shift(west_ref[X_CORNER : X_CORNER + 8, :], 3 - f, 1),
@@ -313,50 +413,44 @@
         line = jnp.where((lane < 64) & (slot >= 3) & (slot <= 12), line, 0.0 if f == 5 else 0.5)
         beyond.append(line)
         for l in range(2):
-            base = 16 * f + l
-            halo_ref[f, pl.ds(l, 8, stride=8), :] = west_ref[pl.ds(base, 8, stride=2), :]
-            halo_ref[f, pl.ds(2 + l, 8, stride=8), :] = east_ref[pl.ds(base, 8, stride=2), :]
-        for r in range(4, 8):
-            halo_ref[f, pl.ds(r, 8, stride=8), :] = line
-
-    windows = []
-    for a in range(3):
-        line = []
-        for b in range(3):
-            line.append(jnp.concatenate(
-                [moved[0][a][b][3:4, :], moved[1][a][b][3:4, :],
-                 moved[0][a][b][12:13, :], moved[1][a][b][12:13, :]] + [rim[b][a]] * 4, 0))
-        windows.append(line)
+            for n, i in enumerate((6, 7)):
+                own = own_ref[pl.ds(8 * l + i, 8, stride=16), :]
+                halo_ref[f, pl.ds(2 * n + l, 8, stride=8), :] = own.astype(F32)
+            east = east_ref[pl.ds(16 * f + l, 8, stride=2), :]
+            halo_ref[f, pl.ds(4 + l, 8, stride=8), :] = east
+            halo_ref[f, pl.ds(6 + l, 8, stride=8), :] = line
+    windows = [
+        [
+            jnp.concatenate(
+                [moved[l][a][b][r : r + 1, :] for r in (3, 4, 5) for l in range(2)]
+                + [rim[b][a]] * 2,
+                0,
+            )
+            for b in range(3)
+        ]
+        for a in range(3)
+    ]
     tiles = [[halo_ref[f, 8 * k : 8 * k + 8, :] for k in range(SD)] for f in range(5)]
     order = [halo_ref[5, 8 * k : 8 * k + 8, :].astype(I32) for k in range(SD)]
-    halo_radius, halo_mult, outer = droplets(windows, *tiles, order)
+    radius, coalesced, outer = droplets(windows, *tiles, order)
     for k in range(SD):
-        table_ref[0, 8 * k : 8 * k + 8, :] = halo_radius[k]
-        table_ref[1, 8 * k : 8 * k + 8, :] = halo_mult[k]
-
-    for side, (ref, dx) in enumerate(((west_ref, 1), (east_ref, -1))):
-        entry = ref[X_LIST : X_LIST + 8, :].astype(I32)
-        live = entry >= 0
-        column = entry & 127
-        group = entry >> 10
-        picked = [jnp.zeros((8, 128), F32) for _ in range(5)]
-        for k in range(SD):
-            for l in range(2):
-                here = live & (group == 2 * k + l)
-                r = 8 * k + 2 * side + l
-                for n in range(5):
-                    src = table_ref if n < 2 else halo_ref
-                    line = jnp.broadcast_to(src[n, r : r + 1, :], (8, 128))
-                    got = jnp.take_along_axis(line, column, axis=1)
-                    picked[n] = jnp.where(here, got, picked[n])
-        box = (((entry >> 10) & 1) * 8 + (((entry >> 7) + dx) & 7)) * 128 + column
-        box = jnp.where(live, box, -1)
-        for c in range(8):
-            at = side * 1024 + c * 128
-            for n in range(5):
-                record_ref[n, 0:1, at : at + 128] = picked[n][c : c + 1, :]
-            box_ref[0:1, at : at + 128] = box[c : c + 1, :]
-
+        table_ref[0, 8 * k : 8 * k + 8, :] = radius[k]
+        table_ref[1, 8 * k : 8 * k + 8, :] = coalesced[k]
+
+    size_ref[...] = early_size[...]
+    mult_ref[...] = early_mult[...]
+    for l in range(2):
+        for n, i in enumerate((6, 7)):
+            rows = pl.ds(8 * l + i, 8, stride=16)
+            at = pl.ds(2 * n + l, 8, stride=8)
+            size_ref[rows, :] = table_ref[0, at, :]
+            mult_ref[rows, :] = jnp.where(mask_ref[rows, :] > 0.5, 0.0, table_ref[1, at, :])
+    leaving[2].start()
+    leaving[3].start()
+
+    face_records(
+        east_ref[X_LIST : X_LIST + 8, :], -1, 4, table_ref, halo_ref, record_ref, box_ref
+    )
     diagonal = lane >= 96
     by_west = diagonal & (lane % 16 < 8)
     entry = jnp.where(
@@ -375,64 +469,40 @@
     dx = jnp.where(diagonal, jnp.where(by_west, 1, -1), 0)
     dy = jnp.where(north_side, -1, 1)
     box = (level * 8 + ((i + dx) & 7)) * 128 + ((column + dy) & 127)
-    box_ref[0:1, 2048:2176] = jnp.where(live, box, -1)[0:1, :]
+    box_ref[0:1, 1024:1152] = jnp.where(live, box, -1)[0:1, :]
     for n in range(5):
-        if n < 2:
-            table = table_ref[n, pl.ds(4, 8, stride=8), :]
-        else:
-            table = beyond[n]
+        table = table_ref[n, pl.ds(6, 8, stride=8), :] if n < 2 else beyond[n]
         got = jnp.take_along_axis(table, at, axis=1)
         line = jnp.sum(jnp.where(mine, got, 0.0), axis=0, keepdims=True)
-        record_ref[n, 0:1, 2048:2176] = line
+        record_ref[n, 0:1, 1024:1152] = line
     leaving[4].start()
     leaving[5].start()
 
-    deposits = []
-    for l in range(2):
-        windows = [[moved[l][a][b][4:12, :] for b in range(3)] for a in range(3)]
-        tiles = [
-            [ref[k * 16 + 8 * l : k * 16 + 8 * l + 8, :] for k in range(SD)]
-            for ref in (sz_ref, wt_ref, dn_ref, ox_ref, oy_ref, pm_ref)
-        ]
-        radius, coalesced, deposit = droplets(windows, *tiles)
-        for k in range(SD):
-            rows = slice(k * 16 + 8 * l, k * 16 + 8 * l + 8)
-            size_ref[rows, :] = radius[k]
-            mult_ref[rows, :] = jnp.where(mask_ref[rows, :] > 0.5, 0.0, coalesced[k])
-        deposits.append(deposit)
-    leaving[2].start()
-    leaving[3].start()
-
-    def along_y(d, a):
-        return (
-            d[a][1]
-            + jnp.where(lane == 0, 0.0, shift(d[a][2], 1, 1))
-            + jnp.where(lane == 127, 0.0, shift(d[a][0], -1, 1))
-        )
-
-    from_west = along_y(outer, 2)
-    from_east = along_y(outer, 0)
-    rim_line = [jnp.where(lane1 < 32, outer[a][2][4:5, :], outer[a][0][4:5, :]) for a in range(3)]
+    down, level_row, up = (along_y(outer, a) for a in range(3))
+    rim_line = [jnp.where(lane1 < 32, outer[a][2][6:7, :], outer[a][0][6:7, :]) for a in range(3)]
     rim_line = shift(rim_line[2], 1, 1) + rim_line[1] + shift(rim_line[0], -1, 1)
     rim_line = jnp.broadcast_to(rim_line, (8, 128))
     for l in range(2):
-        own = [along_y(deposits[l], a) for a in range(3)]
-        west_row = jnp.broadcast_to(from_west[l : l + 1, :], (8, 128))
-        east_row = jnp.broadcast_to(from_east[2 + l : 3 + l, :], (8, 128))
-        source = (
-            own[1]
-            + jnp.where(row8 == 0, west_row, shift(own[2], 1, 0))
-            + jnp.where(row8 == 7, east_row, shift(own[0], -1, 0))
+        extra = (
+            down[l : l + 1, :],
+            level_row[l : l + 1, :] + down[2 + l : 3 + l, :],
+            up[l : l + 1, :] + level_row[2 + l : 3 + l, :] + down[4 + l : 5 + l, :],
         )
+        added = jnp.zeros((8, 128), F32)
+        for r, line in zip((5, 6, 7), extra):
+            added = jnp.where(row8 == r, jnp.broadcast_to(line, (8, 128)), added)
+        rows = slice(8 * l, 8 * l + 8)
+        source = source_ref[rows, :] + added
         for side, j in enumerate((0, 127)):
             wanted = lane == side * 32 + l * 16 + 4 + row8
-            column = jnp.sum(jnp.where(wanted, rim_line, 0.0), axis=1, keepdims=True)
-            source = source + jnp.where(lane == j, column, 0.0)
-        rows = slice(8 * l, 8 * l + 8)
-        moist_ref[rows, :] = mixed[0][l][4:12, :128] - VAPOUR_PER_SOURCE * source
-        warm_ref[rows, :] = mixed[1][l][4:12, :128] + WARMING_FACTOR * source
-    leaving[0].start()
-    leaving[1].start()
+            part = jnp.sum(jnp.where(wanted, rim_line, 0.0), axis=1, keepdims=True)
+            source = source + jnp.where(lane == j, part, 0.0)
+        vapour = jnp.where(row8 < 4, mixed_ref[rows, :], mixed[l][0])
+        warm = jnp.where(row8 < 4, mixed_ref[16 + 8 * l : 24 + 8 * l, :], mixed[l][1])
+        moist_ref[rows, :] = vapour - VAPOUR_PER_SOURCE * source
+        warm_ref[rows, :] = warm + WARMING_FACTOR * source
+    leaving[6].start()
+    leaving[7].start()
     for copy in leaving:
         copy.wait()
 
@@ -514,24 +584,42 @@
     )
     from_west = lax.ppermute(to_east, "gx", ring("gx", 1))
     from_east = lax.ppermute(to_west, "gx", ring("gx", -1))
-    outs = (
-        f32(16, 128),
-        f32(16, 128),
-        f32(128, 128),
-        f32(128, 128),
-        f32(5, 1, 2176),
-        jax.ShapeDtypeStruct((1, 2176), I32),
+    scratch = (pltpu.VMEM((FIELDS, 64, 128), F32), pltpu.VMEM((2, 64, 128), F32))
+    early = call(
+        west_kernel,
+        (
+            pltpu.VMEM((128, 128), F32),
+            pltpu.VMEM((128, 128), F32),
+            pltpu.VMEM((16, 256), F32),
+            pltpu.VMEM((32, 128), F32),
+            pltpu.VMEM((16, 128), F32),
+            pltpu.VMEM((5, 1, 1024), F32),
+            pltpu.VMEM((1, 1024), I32),
+        ),
+        (*given, departed, rim, from_west),
+        scratch=(*scratch, pltpu.VMEM((4, 16, 256), F32)),
     )
     moist, warm, size, mult, records, box = call(
-        physics_kernel,
-        outs,
-        (*given, departed, rim, from_west, from_east),
+        east_kernel,
+        (
+            f32(16, 128),
+            f32(16, 128),
+            f32(128, 128),
+            f32(128, 128),
+            f32(5, 1, 2176),
+            jax.ShapeDtypeStruct((1, 2176), I32),
+        ),
+        (*given, departed, rim, from_west, from_east, *early),
         scratch=(
-            *(pltpu.VMEM(x.shape, x.dtype) for x in outs),
-            pltpu.VMEM((FIELDS, 64, 128), F32),
-            pltpu.VMEM((2, 64, 128), F32),
-            pltpu.VMEM((4, 16, 256), F32),
-            pltpu.SemaphoreType.DMA((6,)),
+            pltpu.VMEM((16, 128), F32),
+            pltpu.VMEM((16, 128), F32),
+            pltpu.VMEM((128, 128), F32),
+            pltpu.VMEM((128, 128), F32),
+            pltpu.VMEM((5, 1, 1152), F32),
+            pltpu.VMEM((1, 1152), I32),
+            *scratch,
+            pltpu.VMEM((4, 8, 256), F32),
+            pltpu.SemaphoreType.DMA((8,)),
         ),
         space=pltpu.HBM,
     )

time: 31.8 us -> 31.5 us (level)
  waiting for transfers between devices: 1.04 us -> 0.03 us
  Pallas kernels: 3.84 us -> 4.51 us
    ppermute x1, waiting for transfers between devices: 1.04 us -> 0.02 us  [per_device(): from_east = lax.ppermute(to_west, 'gx', ring('gx', -1))]
    pallas_call x3 -> x4, Pallas kernels: 2.2 us -> 2.87 us  [call(): pl.pallas_call(kernel, out_shape=outs, in_specs=[pl.BlockSpec(memory_spac...]
  transfers between devices with their start and end apart: 3 -> 3, of which waited for: 1 -> 0; matrix products, arithmetic and copies ran while one was open for 0% -> 0% of each run, Pallas kernels for 1% -> 4%
where the time goes in v4:
time: 31.5 us; the launch traced here: 31.3 us
  starting transfers between devices  20.4 us (65%)
  blocking collectives  5.67 us (18%)
  Pallas kernels  4.51 us (14%)
  between operations  0.68 us (2%)
    ppermute x1, starting transfers between devices, per_device(): from_east = lax.ppermute(to_west, 'gx', ring('gx', -1))  12.6 us
    all_gather x1, blocking collectives, per_device(): lax.all_gather(to_gy, 'gy', axis_index_groups=[[i, i + 1] for i in range(...  5.67 us
    ppermute x1, starting transfers between devices, per_device(): far = lax.ppermute(to_gy, 'gy', swaps('gy', 1))  4.58 us
    ppermute x1, starting transfers between devices, per_device(): from_west = lax.ppermute(to_east, 'gx', ring('gx', 1))  3.19 us
    pallas_call x4, Pallas kernels, call(): pl.pallas_call(kernel, out_shape=outs, in_specs=[pl.BlockSpec(memory_spac...  2.87 us
    pallas_call x1, Pallas kernels, per_device(): pl.pallas_call(pack_gy_kernel, out_shape=(*(pltpu.VMEM(x.shape, x.dtype)...  1.64 us
  transfers between devices with their start and end apart: 3, of which 0 were waited for; matrix products, arithmetic and copies ran while one was open for 0% of the time, Pallas kernels for 4%

profile of v4, /device:TPU:1, one launch (start us, length us, event | category | flops | bytes accessed | tf_op | source)
XLA Modules:
  0.0 31.3 jit_solution(2674402960538952241)
XLA Ops:
  0.6 1.6 %shard_map.154 = (f32[16,128]{1,0:T(8,128)S(1)}, f32[16,128]{1,0:T(8,128)S(1)}, f32[128,128]{1,0:T(8,128)S(1)}, f32[128,128]{1,0:T(8,128)S(1)}, f32[128,128]{1,0...) custom-call(f32[16,128]{1,0:T(8,128)} %bitcast.20, ...), custom_call_target="tpu_custom_call" | custom-call | flops 1048576 | bytes 262144 | tf_op jit(solution)/shard_map/pallas_call | solution.py:563
  2.3 4.6 %collective-permute-start = (f32[56,128]{1,0:T(8,128)S(1)}, f32[56,128]{1,0:T(8,128)S(1)}, u32[]{:S(2)}, u32[]{:S(2)}) collective-permute-start(f32[56,128]{1,0:T(8,128)S(1)} %get-tuple-element.41.g_ref), channel_id=1, source_target_pairs={{1,2},{3,4},{5,6},{7,0},{2,1},{4,3},{6,5},{0,7},{9,10},{11,12},{13... | collective-permute-start | bytes 86024 | tf_op jit(solution)/shard_map/ppermute | solution.py:576
  6.9 5.7 %all-gather = f32[112,128]{1,0:T(8,128)S(1)} all-gather(f32[56,128]{1,0:T(8,128)S(1)} %get-tuple-element.41.g_ref), channel_id=2, replica_groups={{0,1},{2,3},{4,5},{6,7},{8,9},{10,11},{12,13},{14,15},{16,17},{18,19},{..., dimensions={0}, use_global_device_ids=true | all-gather | bytes 86016 | tf_op jit(solution)/shard_map/all_gather | solution.py:578
  12.5 0.0 collective-permute-done.far_ref
  12.6 0.1 shard_map.156
  12.7 3.2 %collective-permute-start.1 = (f32[128,128]{1,0:T(8,128)S(1)}, f32[128,128]{1,0:T(8,128)S(1)}, u32[]{:S(2)}, u32[]{:S(2)}) collective-permute-start(f32[128,128]{1,0:T(8,128)S(1)} %get-tuple-element.43), channel_id=1, source_target_pairs={{0,8},{8,16},{16,24},{24,32},{32,40},{40,48},{48,56},{56,64},{64,7... | collective-permute-start | bytes 196616 | tf_op jit(solution)/shard_map/ppermute | solution.py:585
  15.8 12.6 %collective-permute-start.2 = (f32[128,128]{1,0:T(8,128)S(1)}, f32[128,128]{1,0:T(8,128)S(1)}, u32[]{:S(2)}, u32[]{:S(2)}) collective-permute-start(f32[128,128]{1,0:T(8,128)S(1)} %get-tuple-element.44), channel_id=1, source_target_pairs={{0,504},{8,0},{16,8},{24,16},{32,24},{40,32},{48,40},{56,48},{64,5... | collective-permute-start | bytes 196616 | tf_op jit(solution)/shard_map/ppermute | solution.py:586
  28.4 0.3 shard_map.155.mask_ref
  28.7 0.0 collective-permute-done.1.west_ref
  28.7 1.0 %shard_map.157 = (f32[128,128]{1,0:T(8,128)S(1)}, f32[128,128]{1,0:T(8,128)S(1)}, f32[16,256]{1,0:T(8,128)S(1)}, f32[32,128]{1,0:T(8,128)S(1)}, f32[16,128]{1,0:...) custom-call(f32[16,128]{1,0:T(8,128)S(1)} %get-tuple-element.32.q_ref, ...), custom_call_target="tpu_custom_call" | custom-call | flops 1048576 | bytes 262144 | tf_op jit(solution)/shard_map/pallas_call | solution.py:511
  29.7 0.0 collective-permute-done.2.east_ref
  29.8 1.5 %shard_map.158 = (f32[16,128]{1,0:T(8,128)}, f32[16,128]{1,0:T(8,128)}, f32[128,128]{1,0:T(8,128)}, f32[128,128]{1,0:T(8,128)}, f32[5,1,2176]{2,1,0:T(1,128)}, /*index=5*/s32[1,2176]{1,0:T(1,128)}) custom-call(f32[16,128]{1,0:T(8,128)S(1)} %get-tuple-element.32.q_ref, f32[16,128]{1,0:T(8,128)S(1)} %get-tuple-element.33.t_ref, ...), custom_call_target="tpu_custom_call" | custom-call | flops 1048576 | bytes 262144 | tf_op jit(solution)/shard_map/pallas_call | solution.py:511
Async XLA Ops:
  2.3 10.3 %collective-permute-start = (f32[56,128]{1,0:T(8,128)S(1)}, f32[56,128]{1,0:T(8,128)S(1)}, u32[]{:S(2)}, u32[]{:S(2)}) collective-permute-start(f32[56,128]{1,0:T(8,128)S(1)} %get-tuple-element.41.g_ref), channel_id=1, source_target_pairs={{1,2},{3,4},{5,6},{7,0},{2,1},{4,3},{6,5},{0,7},{9,10},{11,12},{13... | collective-permute-start | bytes 86024 | tf_op jit(solution)/shard_map/ppermute | solution.py:576
  12.7 16.1 %collective-permute-start.1 = (f32[128,128]{1,0:T(8,128)S(1)}, f32[128,128]{1,0:T(8,128)S(1)}, u32[]{:S(2)}, u32[]{:S(2)}) collective-permute-start(f32[128,128]{1,0:T(8,128)S(1)} %get-tuple-element.43), channel_id=1, source_target_pairs={{0,8},{8,16},{16,24},{24,32},{32,40},{40,48},{48,56},{56,64},{64,7... | collective-permute-start | bytes 196616 | tf_op jit(solution)/shard_map/ppermute | solution.py:585
  15.8 13.9 %collective-permute-start.2 = (f32[128,128]{1,0:T(8,128)S(1)}, f32[128,128]{1,0:T(8,128)S(1)}, u32[]{:S(2)}, u32[]{:S(2)}) collective-permute-start(f32[128,128]{1,0:T(8,128)S(1)} %get-tuple-element.44), channel_id=1, source_target_pairs={{0,504},{8,0},{16,8},{24,16},{32,24},{40,32},{48,40},{56,48},{64,5... | collective-permute-start | bytes 196616 | tf_op jit(solution)/shard_map/ppermute | solution.py:586

commit v5 on v4

--- a/solution.py
+++ b/solution.py
@@ -24,8 +24,11 @@
 
 G_LIST = 8 * FIELDS
 G_ROWS = G_LIST + 8
+R_EXT = G_ROWS
+R_ROWS = R_EXT + 32
 X_AIR = 16 * FIELDS
-X_CORNER = X_AIR + 16
+X_EXT = X_AIR + 16
+X_CORNER = X_EXT + 16
 X_LIST = X_CORNER + 8
 X_ROWS = X_LIST + 8
 
@@ -65,18 +68,18 @@
     low_level = lane % 32 < 16
     for f in range(FIELDS):
         ref = kept[2 + f]
-        parts = [ref[k * 16 : k * 16 + 16, :] for k in range(SD - 1, -1, -1)]
+        parts = [ref[k * 16 : k * 16 + 16, :] for k in (0, 7, 6, 5, 4, 3, 2, 1)]
         block = jnp.concatenate(parts, 0)
         if f == 5:
             block = block.astype(F32)
         turned = jnp.transpose(block)
         out = []
-        for base, row in ((0, 127), (32, 0)):
+        for row in (127, 0):
             line = jnp.broadcast_to(turned[row : row + 1, :], (8, 128))
-            line = pltpu.roll(line, 16, 1, stride=16, stride_axis=0)
-            lev0 = pltpu.roll(line, base + 4, 1)
-            lev1 = pltpu.roll(line, base + 12, 1)
+            lev0 = pltpu.roll(line, 4, 1, stride=16, stride_axis=0)
+            lev1 = pltpu.roll(line, 12, 1, stride=16, stride_axis=0)
             out.append(jnp.where(low_level, lev0, lev1))
+        out[1] = shift(out[1], -2, 0)
         block = jnp.where(first, out[0], out[1])
         if f < 4:
             air = kept[f // 2][8 * (f % 2) : 8 * (f % 2) + 8, :]
@@ -103,6 +106,9 @@
     near = jnp.where(even, near_ref[1, G_LIST:G_ROWS, :], near_ref[0, G_LIST:G_ROWS, :])
     small = jnp.where(from_near, near, far_ref[G_LIST:G_ROWS, :])
     rim_ref[G_LIST:G_ROWS, :] = small
+    ext = [shift(blocks[g], -67, 1) for g in range(4)]
+    for g in range(4):
+        rim_ref[R_EXT + 8 * g : R_EXT + 8 * g + 8, :] = ext[g]
     drops = (sz_ref, wt_ref, dn_ref, ox_ref, oy_ref, pm_ref)
     for side, (out_ref, i, row) in enumerate(((east_ref, 7, 5), (west_ref, 0, 0))):
         for f, ref in enumerate(drops):
@@ -114,11 +120,10 @@
             ref = (q_ref, t_ref)[g // 2]
             at = 8 * (g % 2) + row
             out_ref[X_AIR + 3 * g : X_AIR + 3 * g + 3, :] = ref[at : at + 3, :]
+            out_ref[X_EXT + 3 * g : X_EXT + 3 * g + 3, :] = ext[g][row : row + 3, :]
         out_ref[X_AIR + 12 : X_AIR + 16, :] = jnp.zeros((4, 128), F32)
+        out_ref[X_EXT + 12 : X_EXT + 16, :] = jnp.zeros((4, 128), F32)
         corner = small
-        for g in range(4):
-            here = (lane >= 64 + 8 * g) & (lane < 72 + 8 * g)
-            corner = jnp.where(here, shift(blocks[g], 8 * g, 1), corner)
         for f in range(FIELDS):
             here = (lane < 64) & (slot == f)
             corner = jnp.where(here, shift(blocks[f], f - 4 - i, 1), corner)
@@ -293,11 +298,11 @@
         for l in range(2):
             g = 2 * a + l
             row = X_AIR + 3 * g
-            side = shift(west_ref[X_CORNER : X_CORNER + 8, :], -67 - 8 * g, 1)
+            far = X_EXT + 3 * g
             air_ref[g, 4:12, :128] = own_ref[8 * l : 8 * l + 8, :]
-            air_ref[g, 4:12, 128:] = shift(rim_ref[8 * g : 8 * g + 8, :], -67, 1)
+            air_ref[g, 4:12, 128:] = rim_ref[R_EXT + 8 * g : R_EXT + 8 * g + 8, :]
             air_ref[g, 1:4, :128] = west_ref[row : row + 3, :]
-            air_ref[g, 1:4, 128:] = side[5:8, :]
+            air_ref[g, 1:4, 128:] = west_ref[far : far + 3, :]
     moved = []
     for l in range(2):
         vapour = mix(air_ref[l], air_ref[1 - l])
@@ -375,29 +380,49 @@
         for l in range(2):
             g = 2 * a + l
             row = X_AIR + 3 * g
-            side = shift(east_ref[X_CORNER : X_CORNER + 8, :], -67 - 8 * g, 1)
+            far = X_EXT + 3 * g
             air_ref[g, 0:5, :128] = own_ref[8 * l + 3 : 8 * l + 8, :]
-            air_ref[g, 0:5, 128:] = shift(rim_ref[8 * g : 8 * g + 8, :], -67, 1)[3:8, :]
+            air_ref[g, 0:5, 128:] = rim_ref[R_EXT + 8 * g + 3 : R_EXT + 8 * g + 8, :]
             air_ref[g, 5:8, :128] = east_ref[row : row + 3, :]
-            air_ref[g, 5:8, 128:] = side[0:3, :]
+            air_ref[g, 5:8, 128:] = east_ref[far : far + 3, :]
     mixed = []
     moved = []
-    turned = []
+    near = []
     for l in range(2):
         vapour = mix(air_ref[l], air_ref[1 - l])
         warm = mix(air_ref[2 + l], air_ref[3 - l])
         mixed.append((shift(vapour[:, :128], 3, 0), shift(warm[:, :128], 3, 0)))
         humid = moisture_excess(vapour, warm)
         moved.append(stencil(humid))
-        whole = jnp.concatenate([humid_ref[8 * l : 8 * l + 8, :], shift(humid, -1, 0)], 0)
-        ahead = shift(whole, 2, 1)
-        tall = lanes_of((16, 128))
-        turned.append(jnp.where(tall < 8, ahead[:, :128], shift(ahead[:, 128:], 8, 1)))
-    strip = jnp.transpose(jnp.concatenate(turned * 4, 0))
+        near.append((humid_ref[8 * l : 8 * l + 8, :], shift(humid, -1, 0)))
+    south = lane < 32
+    upper = lane % 32 >= 16
     rim = []
     for b in range(3):
-        line = jnp.where(lane1 < 32, strip[b : b + 1, :], strip[b + 9 : b + 10, :])
-        rim.append([shift(line, 1, 1), line, shift(line, -1, 1)])
+        spread = []
+        for tile in range(2):
+            levels = []
+            for l in range(2):
+                main, beside = near[l][tile][:, :128], near[l][tile][:, 128:]
+                if b == 1:
+                    got = jnp.take_along_axis(beside, jnp.where(south, 127, 0), axis=1)
+                else:
+                    place = jnp.where(south, 126, 127) if b == 0 else jnp.where(south, 0, 1)
+                    first, second = (beside, main) if b == 0 else (main, beside)
+                    got = jnp.where(
+                        south,
+                        jnp.take_along_axis(first, place, axis=1),
+                        jnp.take_along_axis(second, place, axis=1),
+                    )
+                levels.append(got)
+            spread.append(jnp.where(upper, levels[1], levels[0]))
+        lines = []
+        for a in range(3):
+            wanted = slot + (a - 1)
+            both = jnp.where(row8 == wanted, spread[0], 0.0)
+            both = both + jnp.where(row8 + 8 == wanted, spread[1], 0.0)
+            lines.append(jnp.sum(both, axis=0, keepdims=True))
+        rim.append(lines)
 
     beyond = []
     for f, own_ref in enumerate((sz_ref, wt_ref, dn_ref, ox_ref, oy_ref, pm_ref)):
@@ -480,8 +505,7 @@
 
     down, level_row, up = (along_y(outer, a) for a in range(3))
     rim_line = [jnp.where(lane1 < 32, outer[a][2][6:7, :], outer[a][0][6:7, :]) for a in range(3)]
-    rim_line = shift(rim_line[2], 1, 1) + rim_line[1] + shift(rim_line[0], -1, 1)
-    rim_line = jnp.broadcast_to(rim_line, (8, 128))
+    rim_line = [jnp.broadcast_to(line, (8, 128)) for line in rim_line]
     for l in range(2):
         extra = (
             down[l : l + 1, :],
@@ -494,8 +518,11 @@
         rows = slice(8 * l, 8 * l + 8)
         source = source_ref[rows, :] + added
         for side, j in enumerate((0, 127)):
-            wanted = lane == side * 32 + l * 16 + 4 + row8
-            part = jnp.sum(jnp.where(wanted, rim_line, 0.0), axis=1, keepdims=True)
+            place = side * 32 + l * 16 + 4 + row8
+            part = jnp.where(lane == place - 1, rim_line[2], 0.0)
+            part = jnp.where(lane == place, rim_line[1], part)
+            part = jnp.where(lane == place + 1, rim_line[0], part)
+            part = jnp.sum(part, axis=1, keepdims=True)
             source = source + jnp.where(lane == j, part, 0.0)
         vapour = jnp.where(row8 < 4, mixed_ref[rows, :], mixed[l][0])
         warm = jnp.where(row8 < 4, mixed_ref[16 + 8 * l : 24 + 8 * l, :], mixed[l][1])
@@ -579,7 +606,7 @@
     departed = call(departed_kernel, f32(128, 128), (east_west, to_gy))
     to_east, to_west, rim = call(
         pack_gx_kernel,
-        (f32(X_ROWS, 128), f32(X_ROWS, 128), f32(G_ROWS, 128)),
+        (f32(X_ROWS, 128), f32(X_ROWS, 128), f32(R_ROWS, 128)),
         (*given, east_west, near, far),
     )
     from_west = lax.ppermute(to_east, "gx", ring("gx", 1))

time: 31.5 us -> 31.1 us (0.987)
  Pallas kernels: 4.51 us -> 3.94 us
    pallas_call x4, Pallas kernels: 2.87 us -> 2.55 us  [call(): pl.pallas_call(kernel, out_shape=outs, in_specs=[pl.BlockSpec(memory_spac...]
  transfers between devices with their start and end apart: 3 -> 3, of which waited for: 0 -> 1; matrix products, arithmetic and copies ran while one was open for 0% -> 0% of each run, Pallas kernels for 4% -> 4%
where the time goes in v5:
time: 31.1 us; the launch traced here: 30.8 us
  starting transfers between devices  20.4 us (66%)
  blocking collectives  5.67 us (18%)
  Pallas kernels  3.94 us (13%)
  between operations  0.68 us (2%)
    ppermute x1, starting transfers between devices, per_device(): from_east = lax.ppermute(to_west, 'gx', ring('gx', -1))  12.6 us
    all_gather x1, blocking collectives, per_device(): lax.all_gather(to_gy, 'gy', axis_index_groups=[[i, i + 1] for i in range(...  5.67 us
    ppermute x1, starting transfers between devices, per_device(): far = lax.ppermute(to_gy, 'gy', swaps('gy', 1))  4.58 us
    ppermute x1, starting transfers between devices, per_device(): from_west = lax.ppermute(to_east, 'gx', ring('gx', 1))  3.19 us
    pallas_call x4, Pallas kernels, call(): pl.pallas_call(kernel, out_shape=outs, in_specs=[pl.BlockSpec(memory_spac...  2.55 us
    pallas_call x1, Pallas kernels, per_device(): pl.pallas_call(pack_gy_kernel, out_shape=(*(pltpu.VMEM(x.shape, x.dtype)...  1.39 us
  transfers between devices with their start and end apart: 3, of which 1 were waited for; matrix products, arithmetic and copies ran while one was open for 0% of the time, Pallas kernels for 4%

profile of v5, /device:TPU:1, one launch (start us, length us, event | category | flops | bytes accessed | tf_op | source)
XLA Modules:
  0.0 30.8 jit_solution(11708266204107787976)
XLA Ops:
  0.6 1.4 %shard_map.154 = (f32[16,128]{1,0:T(8,128)S(1)}, f32[16,128]{1,0:T(8,128)S(1)}, f32[128,128]{1,0:T(8,128)S(1)}, f32[128,128]{1,0:T(8,128)S(1)}, f32[128,128]{1,0...) custom-call(f32[16,128]{1,0:T(8,128)} %bitcast.20, ...), custom_call_target="tpu_custom_call" | custom-call | flops 1048576 | bytes 262144 | tf_op jit(solution)/shard_map/pallas_call | solution.py:590
  2.0 4.6 %collective-permute-start = (f32[56,128]{1,0:T(8,128)S(1)}, f32[56,128]{1,0:T(8,128)S(1)}, u32[]{:S(2)}, u32[]{:S(2)}) collective-permute-start(f32[56,128]{1,0:T(8,128)S(1)} %get-tuple-element.41.g_ref), channel_id=1, source_target_pairs={{1,2},{3,4},{5,6},{7,0},{2,1},{4,3},{6,5},{0,7},{9,10},{11,12},{13... | collective-permute-start | bytes 86024 | tf_op jit(solution)/shard_map/ppermute | solution.py:603
  6.6 5.7 %all-gather = f32[112,128]{1,0:T(8,128)S(1)} all-gather(f32[56,128]{1,0:T(8,128)S(1)} %get-tuple-element.41.g_ref), channel_id=2, replica_groups={{0,1},{2,3},{4,5},{6,7},{8,9},{10,11},{12,13},{14,15},{16,17},{18,19},{..., dimensions={0}, use_global_device_ids=true | all-gather | bytes 86016 | tf_op jit(solution)/shard_map/all_gather | solution.py:605
  12.3 0.0 collective-permute-done.far_ref
  12.3 0.1 shard_map.156
  12.4 3.2 %collective-permute-start.1 = (f32[144,128]{1,0:T(8,128)S(1)}, f32[144,128]{1,0:T(8,128)S(1)}, u32[]{:S(2)}, u32[]{:S(2)}) collective-permute-start(f32[144,128]{1,0:T(8,128)S(1)} %get-tuple-element.43), channel_id=1, source_target_pairs={{0,8},{8,16},{16,24},{24,32},{32,40},{40,48},{48,56},{56,64},{64,7... | collective-permute-start | bytes 221192 | tf_op jit(solution)/shard_map/ppermute | solution.py:612
  15.6 12.6 %collective-permute-start.2 = (f32[144,128]{1,0:T(8,128)S(1)}, f32[144,128]{1,0:T(8,128)S(1)}, u32[]{:S(2)}, u32[]{:S(2)}) collective-permute-start(f32[144,128]{1,0:T(8,128)S(1)} %get-tuple-element.44), channel_id=1, source_target_pairs={{0,504},{8,0},{16,8},{24,16},{32,24},{40,32},{48,40},{56,48},{64,5... | collective-permute-start | bytes 221192 | tf_op jit(solution)/shard_map/ppermute | solution.py:613
  28.2 0.3 shard_map.155.mask_ref
  28.5 0.0 collective-permute-done.1.west_ref
  28.5 0.9 %shard_map.157 = (f32[128,128]{1,0:T(8,128)S(1)}, f32[128,128]{1,0:T(8,128)S(1)}, f32[16,256]{1,0:T(8,128)S(1)}, f32[32,128]{1,0:T(8,128)S(1)}, f32[16,128]{1,0:...) custom-call(f32[16,128]{1,0:T(8,128)S(1)} %get-tuple-element.32.q_ref, ...), custom_call_target="tpu_custom_call" | custom-call | flops 1048576 | bytes 262144 | tf_op jit(solution)/shard_map/pallas_call | solution.py:538
  29.4 0.2 collective-permute-done.2.east_ref
  29.6 1.2 %shard_map.158 = (f32[16,128]{1,0:T(8,128)}, f32[16,128]{1,0:T(8,128)}, f32[128,128]{1,0:T(8,128)}, f32[128,128]{1,0:T(8,128)}, f32[5,1,2176]{2,1,0:T(1,128)}, /*index=5*/s32[1,2176]{1,0:T(1,128)}) custom-call(f32[16,128]{1,0:T(8,128)S(1)} %get-tuple-element.32.q_ref, f32[16,128]{1,0:T(8,128)S(1)} %get-tuple-element.33.t_ref, ...), custom_call_target="tpu_custom_call" | custom-call | flops 1048576 | bytes 262144 | tf_op jit(solution)/shard_map/pallas_call | solution.py:538
Async XLA Ops:
  2.0 10.3 %collective-permute-start = (f32[56,128]{1,0:T(8,128)S(1)}, f32[56,128]{1,0:T(8,128)S(1)}, u32[]{:S(2)}, u32[]{:S(2)}) collective-permute-start(f32[56,128]{1,0:T(8,128)S(1)} %get-tuple-element.41.g_ref), channel_id=1, source_target_pairs={{1,2},{3,4},{5,6},{7,0},{2,1},{4,3},{6,5},{0,7},{9,10},{11,12},{13... | collective-permute-start | bytes 86024 | tf_op jit(solution)/shard_map/ppermute | solution.py:603
  12.4 16.1 %collective-permute-start.1 = (f32[144,128]{1,0:T(8,128)S(1)}, f32[144,128]{1,0:T(8,128)S(1)}, u32[]{:S(2)}, u32[]{:S(2)}) collective-permute-start(f32[144,128]{1,0:T(8,128)S(1)} %get-tuple-element.43), channel_id=1, source_target_pairs={{0,8},{8,16},{16,24},{24,32},{32,40},{40,48},{48,56},{56,64},{64,7... | collective-permute-start | bytes 221192 | tf_op jit(solution)/shard_map/ppermute | solution.py:612
  15.6 14.0 %collective-permute-start.2 = (f32[144,128]{1,0:T(8,128)S(1)}, f32[144,128]{1,0:T(8,128)S(1)}, u32[]{:S(2)}, u32[]{:S(2)}) collective-permute-start(f32[144,128]{1,0:T(8,128)S(1)} %get-tuple-element.44), channel_id=1, source_target_pairs={{0,504},{8,0},{16,8},{24,16},{32,24},{40,32},{48,40},{56,48},{64,5... | collective-permute-start | bytes 221192 | tf_op jit(solution)/shard_map/ppermute | solution.py:613
